TPU v7x, 32 devices: a whole 2x2x4 slice. The times are simulated.
32 devices in a mesh: tgt: 8 (over z, y), src: 4 (over x, core).
Axes of the slice: x: 2, y: 2, z: 4, core: 2. Of those that a mesh axis runs over, the one named last changes fastest.
Arguments:
- lattice: int32 [2, 1024], P(None, ('tgt', 'src')), may hold values from 0 to 63, as said below
- material: int32 [1024], P(('tgt', 'src')), may hold values from 0 to 15
- polarizability: float32 [4, 16, 4], replicated, may hold values from -1.2 to 1.2
- wavenumber: float32 [4], replicated, may hold values from 2 to 3.5
- dipoles: bfloat16 [4, 2, 6, 4, 1024], P(None, None, None, None, ('tgt', 'src')), may hold values from -6 to 6
- adjoint_in: bfloat16 [4, 2, 6, 4, 1024], P(None, None, None, None, ('tgt', 'src')), may hold values from -6 to 6
Outputs:
- forward_out: float32 [4, 2, 6, 4, 1024], P(None, None, None, None, ('tgt', 'src'))
- adjoint_out: float32 [4, 2, 6, 4, 1024], P(None, None, None, None, ('tgt', 'src'))
Inputs may be any that keep to these rules, and one draw needn't show every extreme that they name: Atoms are numbered tile by tile, the second tile index fastest; a tile spans 2 x 16 lattice sites, and its 32 atoms occupy each of its sites exactly once, in any order. The first index runs from 0 to 15, the second from 0 to 63.
All inputs are finite; a program needn't handle non-finite values.
Results may differ from a plain program's by a relative error of at most 0.0039.
Values may be sent and summed in bfloat16 or wider, within the bound.
No kernel may reach another device: no remote copies, remote signals or barrier semaphores. Data moves between devices by JAX's collectives and lax.ppermute only.
A program may use at most 64 MiB of HBM per device.

v0:
```python
import jax
import jax.numpy as jnp
from jax import lax
from jax.sharding import PartitionSpec as P

TILE_Y = 16
TILE_X = 2


COUPLINGS = (
    (0, 1, 0, 1.0),
    (0, 3, 1, 1.0),
    (0, 5, 5, 1.0),
    (1, 3, 0, 1.0),
    (1, 2, 1, 1.0),
    (1, 4, 5, -1.0),
    (2, 0, 2, 1.0),
    (2, 4, 4, 1.0),
    (2, 5, 3, -1.0),
    (3, 1, 3, 1.0),
    (3, 3, 4, 1.0),
    (3, 5, 2, -1.0),
    (4, 3, 3, 1.0),
    (4, 2, 4, 1.0),
    (4, 4, 2, 1.0),
    (5, 0, 5, 1.0),
    (5, 4, 1, -1.0),
    (5, 5, 0, 1.0),
)
KERNEL_SOURCES = (
    (0, (2, 5)),
    (1, (0, 3)),
    (2, (1, 4)),
    (3, (0, 1, 3, 4)),
    (4, (1, 2, 4, 5)),
    (5, (0, 2, 3, 5)),
)


def extended(x, sides, width):
    for axis, dim in sides:
        devices, length = (lax.axis_size(axis), x.shape[dim])
        up = [(i, (i + 1) % devices) for i in range(devices)]
        down = [(j, i) for i, j in up]
        last = lax.slice_in_dim(x, length - width, length, axis=dim)
        initial = lax.slice_in_dim(x, 0, width, axis=dim)
        before = lax.ppermute(last, axis, up)
        after = lax.ppermute(initial, axis, down)
        x = jnp.concatenate([before, x, after], axis=dim)
    return x


def atom_polarizability(material, polarizability):
    kinds = jnp.arange(polarizability.shape[1], dtype=jnp.int32)
    onehot = (kinds[:, None] == material[None, :]).astype(jnp.float32)
    table = jnp.einsum("kyw,yn->kwn", polarizability, onehot, precision=lax.Precision.HIGHEST)
    alpha_re = jnp.stack([table[0]] * 3 + [table[2]] * 3, axis=1)[:, :, None, :]
    alpha_im = jnp.stack([table[1]] * 3 + [table[3]] * 3, axis=1)[:, :, None, :]
    return (alpha_re, alpha_im)


def pack_sources(dipoles, adjoint_in, alpha):
    alpha_re, alpha_im = alpha
    vector = adjoint_in.astype(jnp.float32)
    scaled_re = alpha_re * vector[:, 0] + alpha_im * vector[:, 1]
    scaled_im = alpha_re * vector[:, 1] - alpha_im * vector[:, 0]
    scaled = jnp.stack([scaled_re, scaled_im], axis=1).astype(jnp.bfloat16)
    return jnp.stack([dipoles, scaled], axis=1)


def green_kernels(geometry, wave):
    present, radius, unit_x, unit_y = geometry
    phase = wave * radius
    inverse = 1.0 / phase
    weight = present * inverse
    green_re = jnp.cos(phase) * weight
    green_im = jnp.sin(phase) * weight
    inv_sq = inverse * inverse
    near_re = green_re * (1.0 - inv_sq) - green_im * inverse
    near_im = green_im * (1.0 - inv_sq) + green_re * inverse
    long_re = green_re * (3.0 * inv_sq - 1.0) + 3.0 * green_im * inverse
    long_im = green_im * (3.0 * inv_sq - 1.0) - 3.0 * green_re * inverse
    cross_re = green_re - green_im * inverse
    cross_im = green_im + green_re * inverse
    xx_unit = unit_x * unit_x
    yy_unit = unit_y * unit_y
    xy_unit = unit_x * unit_y
    return jnp.stack(
        [
            jnp.stack([near_re, near_im]),
            jnp.stack([near_re + long_re * xx_unit, near_im + long_im * xx_unit]),
            jnp.stack([near_re + long_re * yy_unit, near_im + long_im * yy_unit]),
            jnp.stack([long_re * xy_unit, long_im * xy_unit]),
            jnp.stack([cross_re * unit_x, cross_im * unit_x]),
            jnp.stack([cross_re * unit_y, cross_im * unit_y]),
        ]
    ).astype(jnp.bfloat16)


def kernel_products(values, kernel_pair, kernel_index, components):
    sources = values.shape[-1]
    excite = values.shape[-2]
    targets = kernel_pair.shape[-1]
    count = len(components)
    picked = jnp.stack([values[:, :, comp] for comp in components]).reshape(-1, sources)
    with_re = jnp.dot(picked, kernel_pair[0], preferred_element_type=jnp.float32).reshape(
        count, 2, 2, excite, targets
    )
    with_im = jnp.dot(picked, kernel_pair[1], preferred_element_type=jnp.float32).reshape(
        count, 2, 2, excite, targets
    )
    fwd_re = with_re[:, 0, 0] - with_im[:, 0, 1]
    fwd_im = with_re[:, 0, 1] + with_im[:, 0, 0]
    adj_re = with_re[:, 1, 0] + with_im[:, 1, 1]
    adj_im = with_re[:, 1, 1] - with_im[:, 1, 0]
    if kernel_index >= 4:
        adj_re = -adj_re
        adj_im = -adj_im
    return jnp.stack([fwd_re, fwd_im, adj_re, adj_im], axis=1)


def column_fields(target_sites, source_sites, values, wavenumber, period):
    delta_x = target_sites[0][None, :] - source_sites[0][:, None]
    delta_y = target_sites[1][None, :] - source_sites[1][:, None]
    delta_y = jnp.where(
        2 * delta_y > period,
        delta_y - period,
        jnp.where(2 * delta_y < -period, delta_y + period, delta_y),
    )
    delta_x = delta_x.astype(jnp.float32)
    delta_y = delta_y.astype(jnp.float32)
    radius_sq = delta_x * delta_x + delta_y * delta_y
    present = radius_sq > 0.5
    radius = jnp.sqrt(jnp.where(present, radius_sq, 1.0))
    geometry = (present.astype(jnp.float32), radius, delta_x / radius, delta_y / radius)
    targets = target_sites.shape[1]
    per_wave = []
    for wave_index in range(values.shape[0]):
        kernels = green_kernels(geometry, wavenumber[wave_index])
        products = {}
        for kernel_index, components in KERNEL_SOURCES:
            products[kernel_index] = kernel_products(
                values[wave_index], kernels[kernel_index], kernel_index, components
            )
        outputs = []
        for target_comp in range(6):
            summed = None
            for out_comp, kernel_index, source_comp, sign in COUPLINGS:
                if out_comp == target_comp:
                    place = dict(KERNEL_SOURCES)[kernel_index].index(source_comp)
                    term = sign * products[kernel_index][place]
                    summed = term if summed is None else summed + term
            outputs.append(summed)
        per_wave.append(jnp.stack(outputs, axis=1))
    return jnp.stack(per_wave).reshape(-1, targets)


def finish_outputs(fields, dipoles, adjoint_in, alpha):
    alpha_re, alpha_im = alpha
    shaped = fields.reshape((dipoles.shape[0], 2) + dipoles.shape[1:])
    forward_field = shaped[:, 0]
    adjoint_field = shaped[:, 1]
    source = dipoles.astype(jnp.float32)
    out_re = source[:, 0] - (alpha_re * forward_field[:, 0] - alpha_im * forward_field[:, 1])
    out_im = source[:, 1] - (alpha_re * forward_field[:, 1] + alpha_im * forward_field[:, 0])
    forward_out = jnp.stack([out_re, out_im], axis=1)
    adjoint_out = adjoint_in.astype(jnp.float32) - adjoint_field
    return (forward_out, adjoint_out)


def per_device(lattice, material, polarizability, wavenumber, dipoles, adjoint_in):
    atoms = lattice.shape[1]
    columns = lax.axis_size("src")
    band = lax.axis_index("tgt")
    column = lax.axis_index("src")
    period = columns * TILE_Y
    alpha = atom_polarizability(material, polarizability)
    values = pack_sources(dipoles, adjoint_in, alpha)
    value_shape = values.shape[:-1]
    offsets = jnp.stack([lattice[0] - band * TILE_X, lattice[1] - column * TILE_Y]).astype(
        jnp.bfloat16
    )
    payload = jnp.concatenate([values.reshape(-1, atoms), offsets], axis=0)
    widened = extended(payload, (("src", 1),), atoms)
    piece = lax.all_gather(widened, "tgt", axis=1, tiled=True)
    count = piece.shape[1]
    position = jnp.arange(count, dtype=jnp.int32)
    source_band = position // (3 * atoms)
    neighbour = position % (3 * atoms) // atoms
    local_sites = piece[-2:].astype(jnp.int32)
    source_sites = jnp.stack(
        [
            source_band * TILE_X + local_sites[0],
            (column + neighbour + columns - 1) % columns * TILE_Y + local_sites[1],
        ]
    )
    source_values = piece[:-2].reshape(value_shape + (count,))
    fields = column_fields(lattice, source_sites, source_values, wavenumber, period)
    return finish_outputs(fields, dipoles, adjoint_in, alpha)


def solution(mesh):
    in_specs = (
        P(None, ("tgt", "src")),
        P(("tgt", "src")),
        P(),
        P(),
        P(None, None, None, None, ("tgt", "src")),
        P(None, None, None, None, ("tgt", "src")),
    )
    out_specs = (
        P(None, None, None, None, ("tgt", "src")),
        P(None, None, None, None, ("tgt", "src")),
    )
    return jax.shard_map(
        per_device, mesh=mesh, in_specs=in_specs, out_specs=out_specs, check_vma=False
    )
```

profile of v0, /device:TPU:0, one launch (start us, length us, event | category | flops | bytes accessed | tf_op | source)
XLA Modules:
  0.0 61.9 jit_solution(14754434010374544946)
XLA Ops:
  0.6 0.8 %copy_convert_fusion = f32[4,2,6,4,32]{4,3,2,0,1:T(4,128)S(1)} fusion(bf16[4,2,6,4,32]{4,3,2,1,0:T(4,128)(2,1)} %param.11), kind=kLoop, calls=%fused_computation.333 | loop fusion | flops 6144 | bytes 36864 | tf_op jit(solution)/shard_map/convert_element_type | solution.py:64
  1.5 0.6 %copy-done.5 = s32[32]{0:T(128)S(1)} copy-done((s32[32]{0:T(128)S(1)}, s32[32]{0:T(128)}, u32[]{:S(2)}) %copy-start.5) | copy-done | bytes 152
  2.5 0.6 %copy-done.4 = s32[2,32]{1,0:T(2,128)S(1)} copy-done((s32[2,32]{1,0:T(2,128)S(1)}, s32[2,32]{1,0:T(2,128)}, u32[]{:S(2)}) %copy-start.4) | copy-done | bytes 280
  3.3 0.6 copy-done.1
  4.3 2.4 %collective-permute-start.1 = (bf16[386,32]{0,1:T(8,128)(2,1)S(1)}, bf16[386,32]{0,1:T(8,128)(2,1)S(1)}, u32[]{:S(2)}, u32[]{:S(2)}) collective-permute-start(bf16[386,32]{0,1:T(8,128)(2,1)S(1)} %pad_maximum_fusion.43), channel_id=1, source_target_pairs={{1,0},{2,1},{3,2},{0,3},{5,4},{6,5},{7,6},{4,7},{9,8},{10,9},{11,1... | collective-permute-start | bytes 74120 | tf_op jit(solution)/shard_map/ppermute | solution.py:48
  6.7 0.7 %fusion.280 = (f32[1]{0:T(128)}, f32[1]{0:T(128)}, f32[1]{0:T(128)}, f32[1]{0:T(128)}) fusion(f32[4]{0:T(128)S(1)} %copy-done.3), kind=kLoop, calls=%fused_computation.740 | loop fusion | bytes 32 | tf_op jit(solution)/shard_map/slice | solution.py:139
  7.3 1.1 %collective-permute-done.1 = bf16[386,32]{0,1:T(8,128)(2,1)S(1)} collective-permute-done((bf16[386,32]{0,1:T(8,128)(2,1)S(1)}, bf16[386,32]{0,1:T(8,128)(2,1)S(1)}, u32[]{:S(2)}, u32[]{:S(2)}) %collective-permute-start.1) | collective-permute-done | bytes 24736 | tf_op jit(solution)/shard_map/ppermute | solution.py:48
  8.4 1.6 %collective-permute-done = bf16[386,32]{0,1:T(8,128)(2,1)S(1)} collective-permute-done((bf16[386,32]{0,1:T(8,128)(2,1)S(1)}, bf16[386,32]{0,1:T(8,128)(2,1)S(1)}, u32[]{:S(2)}, u32[]{:S(2)}) %collective-permute-start) | collective-permute-done | bytes 24736 | tf_op jit(solution)/shard_map/ppermute | solution.py:47
  10.1 32.6 %all_gather.3 = bf16[386,768]{0,1:T(8,128)(2,1)S(1)} all-gather(bf16[386,96]{0,1:T(8,128)(2,1)S(1)} %pad_maximum_fusion.29), channel_id=1, replica_groups=mesh['tgt'=8,'src'=4] {'tgt'}, dimensions={1}, use_global_device_ids=true | all-gather | bytes 667008 | tf_op jit(solution)/shard_map/all_gather | solution.py:185
  42.7 0.2 fusion.279
  43.2 0.4 slice_reduce_fusion.1
  43.7 4.7 %fusion.271 = (bf16[1,768,32]{1,2,0:T(8,128)(2,1)S(1)}, bf16[1,768,32]{1,2,0:T(8,128)(2,1)S(1)}, bf16[1,768,32]{1,2,0:T(8,128)(2,1)S(1)}, bf16[1,768,32]{1,2,0:T...) fusion(s32[768]{0:T(1024)S(1)} %fusion.210, ...), kind=kLoop, calls=%fused_computation.731 | loop fusion | flops 5529600 | bytes 2365712 | tf_op jit(solution)/shard_map/convert.94
  48.4 0.1 pad_maximum_fusion.26
  48.6 0.2 fusion.18
  48.7 0.2 fusion.20
  48.9 0.2 fusion.14
  49.1 0.2 fusion.16
  49.3 0.1 fusion.67
  49.5 0.1 fusion.68
  49.7 0.1 fusion.69
  49.8 0.1 fusion.70
  50.0 0.2 fusion.22
  50.2 0.2 fusion.24
  50.4 0.1 fusion.71
  50.6 0.1 fusion.72
  51.0 0.1 pad_maximum_fusion.19
  51.1 0.2 fusion.30
  51.3 0.2 fusion.32
  51.5 0.2 fusion.26
  51.7 0.2 fusion.28
  51.9 0.1 fusion.73
  52.0 0.1 fusion.74
  52.3 0.1 fusion.75
  52.4 0.1 fusion.76
  52.6 0.2 fusion.34
  52.7 0.2 fusion.36
  53.0 0.1 fusion.77
  53.1 0.1 fusion.78
  53.5 0.1 pad_maximum_fusion.12
  53.7 0.2 fusion.42
  53.9 0.2 fusion.44
  54.1 0.2 fusion.38
  54.2 0.2 fusion.40
  54.5 0.1 fusion.79
  54.8 0.1 fusion.81
  55.0 0.1 fusion.82
  55.1 0.2 fusion.46
  55.3 0.2 fusion.48
  55.5 0.1 fusion.83
  55.7 0.1 fusion.84
  56.1 0.1 pad_maximum_fusion.5
  56.3 0.2 fusion.54
  56.4 0.2 fusion.56
  56.6 0.2 fusion.50
  56.8 0.2 fusion.52
  57.0 0.1 fusion.85
  57.4 0.1 fusion.87
  57.7 0.2 fusion.58
  57.9 0.2 fusion.60
  58.0 0.2 fusion.89
  58.2 0.2 fusion.90
  59.8 0.8 %copy-done.2 = bf16[4,2,6,4,32]{4,3,2,1,0:T(4,128)(2,1)S(1)} copy-done((bf16[4,2,6,4,32]{4,3,2,1,0:T(4,128)(2,1)S(1)}, bf16[4,2,6,4,32]{4,3,2,1,0:T(4,128)(2,1)}, u32[]{:S(2)}) %copy-start.2) | copy-done | bytes 12312
  60.5 0.7 %fusion.12 = f32[4,2,6,4,32]{4,3,2,1,0:T(4,128)} fusion(f32[4,2,2,6,4,32]{5,4,3,2,0,1:T(4,128)S(1)} %pad_maximum_fusion, bf16[4,2,6,4,32]{4,3,2,1,0:T(4,128)(2,1)S(1)} %copy-done.2), kind=kLoop, calls=%fused_computation.49 | loop fusion | flops 12288 | bytes 61440 | tf_op jit(solution)/shard_map/sub | solution.py:167
  61.2 0.7 %pad_maximum_fusion.30 = f32[4,2,6,4,32]{4,3,2,1,0:T(4,128)} fusion(f32[4,1,6,4,32]{4,3,2,1,0:T(4,128)S(1)} %get-tuple-element.9, f32[4,1,6,4,32]{4,3,2,1,0:T(4,128)S(1)} %get-tuple-element.8), kind=kLoop, calls=%fused_computation.77 | loop fusion | flops 6144 | bytes 49152 | tf_op jit(solution)/shard_map/stack | solution.py:166
  (168 shorter events, 4.0 us)
Async XLA Ops:
  0.6 0.8 %copy-start = (f32[4,16,4]{1,2,0:T(4,128)S(1)}, f32[4,16,4]{1,2,0:T(4,128)}, u32[]{:S(2)}) copy-start(f32[4,16,4]{1,2,0:T(4,128)} %param.8) | copy-start | bytes 3076
  1.5 0.7 %copy-start.5 = (s32[32]{0:T(128)S(1)}, s32[32]{0:T(128)}, u32[]{:S(2)}) copy-start(s32[32]{0:T(128)} %param.7) | copy-start | bytes 388
  2.4 0.7 %copy-start.4 = (s32[2,32]{1,0:T(2,128)S(1)}, s32[2,32]{1,0:T(2,128)}, u32[]{:S(2)}) copy-start(s32[2,32]{1,0:T(2,128)} %param.6) | copy-start | bytes 772
  3.1 0.8 %copy-start.1 = (bf16[4,2,6,4,32]{4,3,2,1,0:T(4,128)(2,1)S(1)}, bf16[4,2,6,4,32]{4,3,2,1,0:T(4,128)(2,1)}, u32[]{:S(2)}) copy-start(bf16[4,2,6,4,32]{4,3,2,1,0:T(4,128)(2,1)} %param.10) | copy-start | bytes 36868
  4.2 2.5 %copy-start.3 = (f32[4]{0:T(128)S(1)}, f32[4]{0:T(128)}, u32[]{:S(2)}) copy-start(f32[4]{0:T(128)} %param.9) | copy-start | bytes 52
  4.3 4.1 %collective-permute-start.1 = (bf16[386,32]{0,1:T(8,128)(2,1)S(1)}, bf16[386,32]{0,1:T(8,128)(2,1)S(1)}, u32[]{:S(2)}, u32[]{:S(2)}) collective-permute-start(bf16[386,32]{0,1:T(8,128)(2,1)S(1)} %pad_maximum_fusion.43), channel_id=1, source_target_pairs={{1,0},{2,1},{3,2},{0,3},{5,4},{6,5},{7,6},{4,7},{9,8},{10,9},{11,1... | collective-permute-start | bytes 74120 | tf_op jit(solution)/shard_map/ppermute | solution.py:48
  6.7 3.3 %collective-permute-start = (bf16[386,32]{0,1:T(8,128)(2,1)S(1)}, bf16[386,32]{0,1:T(8,128)(2,1)S(1)}, u32[]{:S(2)}, u32[]{:S(2)}) collective-permute-start(bf16[386,32]{0,1:T(8,128)(2,1)S(1)} %pad_maximum_fusion.43), channel_id=1, source_target_pairs={{0,1},{1,2},{2,3},{3,0},{4,5},{5,6},{6,7},{7,4},{8,9},{9,10},{10,1... | collective-permute-start | bytes 74120 | tf_op jit(solution)/shard_map/ppermute | solution.py:47
  59.7 0.8 %copy-start.2 = (bf16[4,2,6,4,32]{4,3,2,1,0:T(4,128)(2,1)S(1)}, bf16[4,2,6,4,32]{4,3,2,1,0:T(4,128)(2,1)}, u32[]{:S(2)}) copy-start(bf16[4,2,6,4,32]{4,3,2,1,0:T(4,128)(2,1)} %param.11) | copy-start | bytes 36868
where the time goes:
time: 62.3 us; the launch traced here: 61.9 us
  blocking collectives  32.6 us (52%)
  other arithmetic  9.25 us (15%)
  matrix products  7.54 us (12%)
  local copies, waits for them, and re-layouts  5.54 us (9%)
  waiting for transfers between devices  2.67 us (4%)
  starting transfers between devices  2.41 us (4%)
  between operations  1.89 us (3%)
    all_gather x1, blocking collectives, per_device(): piece = lax.all_gather(widened, 'tgt', axis=1, tiled=True)  32.6 us
    another operation x2, other arithmetic  4.71 us
    dot_general x24, matrix products, kernel_products(): jnp.dot(picked, kernel_pair[1], preferred_element_type=jnp.float32)  3.71 us
    dot_general x24, matrix products, kernel_products(): jnp.dot(picked, kernel_pair[0], preferred_element_type=jnp.float32)  3.7 us
    unnamed x43, local copies, waits for them, and re-layouts  3.13 us
    ppermute x1, starting transfers between devices, extended(): after = lax.ppermute(initial, axis, down)  2.41 us
    ppermute x1, waiting for transfers between devices, extended(): before = lax.ppermute(last, axis, up)  1.6 us
  transfers between devices with their start and end apart: 2, of which 2 were waited for; matrix products, arithmetic and copies ran while one was open for 1% of the time, Pallas kernels for 0%

commit v1 on v0

v1 whole, which is shorter than its diff:
```python
import functools

import jax
import jax.numpy as jnp
from jax import lax
from jax.experimental import pallas as pl
from jax.experimental.pallas import tpu as pltpu
from jax.sharding import PartitionSpec as P

TILE_Y = 16
TILE_X = 2
ATOMS = TILE_X * TILE_Y
AXES = ("tgt", "src")
BANDS = 2

SETS = ((0, 1, 5), (3, 4, 2))
PLACES = (((0, 0),), ((1, 1),), ((2, 2),), ((1, 0), (0, 1)), ((2, 0), (0, 2)), ((2, 1), (1, 2)))


def z_partner(z, shift, count):
    return z ^ shift if count & (count - 1) == 0 else (z + shift) % count


def column_partner(s, slot, count):
    if slot == 0:
        return s
    if count % 2:
        return (s + (1 if slot == 1 else -1)) % count
    step = 1 if (s % 2 == 0) == (slot == 1) else -1
    return (s + step) % count


def pairs(n_tgt, n_src, shift, flip, slot):
    depth = n_tgt // BANDS
    out = []
    for t in range(n_tgt):
        z, y = divmod(t, BANDS)
        for s in range(n_src):
            to_t = z_partner(z, shift, depth) * BANDS + (y + flip) % BANDS
            out.append((t * n_src + s, to_t * n_src + column_partner(s, slot, n_src)))
    return out


def site_of(lattice):
    return (lattice[0:1] % TILE_X) * TILE_Y + lattice[1:2] % TILE_Y


def pack_kernel(lattice_ref, material_ref, pol_ref, dip_ref, adj_ref, payload_ref, alpha_ref):
    waves, _, _, excite, atoms = dip_ref.shape
    types = pol_ref.shape[2]
    kinds = lax.broadcasted_iota(jnp.int32, (types, atoms), 0)
    onehot = jnp.where(kinds == material_ref[...], 1.0, 0.0).astype(jnp.float32)
    alpha = []
    for kind in range(4):
        value = jnp.dot(
            pol_ref[kind], onehot, precision=lax.Precision.HIGHEST, preferred_element_type=jnp.float32
        )
        alpha_ref[kind] = value
        alpha.append(value)
    rows = []
    for w in range(waves):
        fwd = {}
        adj = {}
        for comp in range(6):
            base = 0 if comp < 3 else 2
            a_re = alpha[base][w : w + 1]
            a_im = alpha[base + 1][w : w + 1]
            v_re = adj_ref[w, 0, comp].astype(jnp.float32)
            v_im = adj_ref[w, 1, comp].astype(jnp.float32)
            fwd[comp] = (dip_ref[w, 0, comp].astype(jnp.float32), dip_ref[w, 1, comp].astype(jnp.float32))
            adj[comp] = (a_re * v_re + a_im * v_im, a_re * v_im - a_im * v_re)
        for c in range(3):
            first, second = SETS[0][c], SETS[1][c]
            for ri in range(2):
                f1 = fwd[first][ri]
                f2 = fwd[second][ri] if c < 2 else -fwd[second][ri]
                a1 = adj[first][ri]
                a2 = adj[second][ri]
                if ri == 1:
                    a1, a2 = -a1, -a2
                if c == 2:
                    a1 = -a1
                rows += [f1, f2, a1, a2]
    table = jnp.concatenate(rows, axis=0).astype(jnp.bfloat16)
    sites = lax.broadcasted_iota(jnp.int32, (atoms, atoms), 0)
    place = jnp.where(sites == site_of(lattice_ref[...]), 1.0, 0.0).astype(jnp.bfloat16)
    payload_ref[...] = lax.dot_general(
        place, table, (((1,), (1,)), ((), ())), preferred_element_type=jnp.float32
    ).astype(jnp.bfloat16)


def sin_cos(x):
    turns = jnp.floor(x * 0.6366197723675814 + 0.5)
    rest = ((x - turns * 1.5703125) - turns * 4.837512969970703125e-4) - turns * 7.54978995489188216e-8
    sq = rest * rest
    sin = rest + rest * sq * (-1.6666654611e-1 + sq * (8.3321608736e-3 - sq * 1.9515295891e-4))
    cos = 1.0 - 0.5 * sq + sq * sq * (4.166664568298827e-2 + sq * (-1.388731625493765e-3 + sq * 2.443315711809948e-5))
    quarter = turns.astype(jnp.int32)
    odd = (quarter & 1) == 1
    sin, cos = jnp.where(odd, cos, sin), jnp.where(odd, sin, cos)
    sin = jnp.where((quarter & 2) == 2, -sin, sin)
    cos = jnp.where(((quarter + 1) & 2) == 2, -cos, cos)
    return sin, cos


def green_kernel(wave_ref, out_ref, *, n_tgt, n_src):
    waves, _, double, targets = out_ref.shape
    sources = double // 2
    depth = n_tgt // BANDS
    band = lax.axis_index("tgt")
    column = lax.axis_index("src")
    z, y = band // BANDS, band % BANDS
    period = n_src * TILE_Y
    if n_src % 2:
        step = 1
    else:
        step = 1 - 2 * (column % 2)
    lane = lax.broadcasted_iota(jnp.int32, (1, targets), 1)
    slot = lane // (BANDS * ATOMS)
    offset = jnp.where(slot == 0, 0, jnp.where(slot == 1, step, -step))
    to_band = z * BANDS + (y + lane // ATOMS) % BANDS
    to_x = to_band * TILE_X + lane % ATOMS // TILE_Y
    to_y = offset * TILE_Y + lane % TILE_Y
    for k in range(depth):
        from_band = z_partner(z, k, depth) * BANDS + y
        row = lax.broadcasted_iota(jnp.int32, (ATOMS, 1), 0)
        dx = to_x - (from_band * TILE_X + row // TILE_Y)
        dy = to_y - row % TILE_Y
        dy = jnp.where(2 * dy > period, dy - period, jnp.where(2 * dy < -period, dy + period, dy))
        dx = dx.astype(jnp.float32)
        dy = dy.astype(jnp.float32)
        square = dx * dx + dy * dy
        inverse = jnp.where(square > 0.5, lax.rsqrt(jnp.maximum(square, 1.0)), 0.0)
        radius = square * inverse
        ux = dx * inverse
        uy = dy * inverse
        xx, yy, xy = ux * ux, uy * uy, ux * uy
        ux = -ux
        for w in range(waves):
            wave = wave_ref[w]
            sin, cos = sin_cos(wave * radius)
            inv = inverse * (1.0 / wave)
            g_re = cos * inv
            g_im = sin * inv
            h_re = g_re * inv
            h_im = g_im * inv
            e_re = h_re * inv + h_im
            e_im = h_im * inv - h_re
            near = (g_re - e_re, g_im - e_im)
            far = (3.0 * e_re - g_re, 3.0 * e_im - g_im)
            cross = (g_re - h_im, g_im + h_re)
            for part in range(2):
                there = pl.ds(part * sources + k * ATOMS, ATOMS)
                n, f, c = near[part], far[part], cross[part]
                out_ref[w, 0, there] = (n + f * xx).astype(jnp.bfloat16)
                out_ref[w, 1, there] = (n + f * yy).astype(jnp.bfloat16)
                out_ref[w, 2, there] = n.astype(jnp.bfloat16)
                out_ref[w, 3, there] = (f * xy).astype(jnp.bfloat16)
                out_ref[w, 4, there] = (c * uy).astype(jnp.bfloat16)
                out_ref[w, 5, there] = (c * ux).astype(jnp.bfloat16)


def field_kernel(*refs):
    *tile_refs, kernels_ref, own_ref, sent_ref = refs
    waves = kernels_ref.shape[0]
    gathered = jnp.concatenate([ref[...].astype(jnp.float32) for ref in tile_refs], axis=0)
    rows = gathered.T.astype(jnp.bfloat16)
    half = rows.shape[0] // (waves * 6)
    fields = []
    for w in range(waves):
        left = []
        for c in range(3):
            base = (w * 3 + c) * 2 * half
            re, im = rows[base : base + half], rows[base + half : base + 2 * half]
            left.append(
                jnp.concatenate(
                    [jnp.concatenate([re, -im], axis=1), jnp.concatenate([im, re], axis=1)], axis=0
                )
            )
        total = [None] * 3
        for index, places in enumerate(PLACES):
            stacked = jnp.concatenate([left[c_in] for c_in, _ in places], axis=0)
            product = jnp.dot(stacked, kernels_ref[w, index], preferred_element_type=jnp.float32)
            for number, (_, c_out) in enumerate(places):
                piece = product[number * 2 * half : (number + 1) * 2 * half]
                total[c_out] = piece if total[c_out] is None else total[c_out] + piece
        fields += total
    turned = jnp.concatenate(fields, axis=0).T
    own_ref[...] = turned[:ATOMS]
    for index in range(sent_ref.shape[0]):
        sent_ref[index] = turned[(index + 1) * ATOMS : (index + 2) * ATOMS].astype(jnp.bfloat16)


def finish_kernel(*refs):
    lattice_ref, alpha_ref, dip_ref, adj_ref, own_ref, *rest = refs
    *got_refs, fwd_ref, out_ref = rest
    waves, _, _, excite, atoms = dip_ref.shape
    field = own_ref[...]
    for ref in got_refs:
        field = field + ref[...].astype(jnp.float32)
    high = field.astype(jnp.bfloat16)
    low = (field - high.astype(jnp.float32)).astype(jnp.bfloat16)
    sites = lax.broadcasted_iota(jnp.int32, (atoms, atoms), 0)
    place = jnp.where(sites == site_of(lattice_ref[...]), 1.0, 0.0).astype(jnp.bfloat16)
    rows = lax.dot_general(
        jnp.concatenate([high, low], axis=0),
        jnp.concatenate([place, place], axis=0),
        (((0,), (0,)), ((), ())),
        preferred_element_type=jnp.float32,
    )
    for w in range(waves):
        for c in range(3):
            base = (w * 3 + c) * 8 * excite
            pick = lambda ri, fa, which: rows[base + ((ri * 2 + fa) * 2 + which) * excite :][:excite]
            for which in range(2):
                comp = SETS[which][c]
                kind = 0 if comp < 3 else 2
                a_re = alpha_ref[kind, w : w + 1]
                a_im = alpha_ref[kind + 1, w : w + 1]
                f_re, f_im = pick(0, 0, which), pick(1, 0, which)
                if comp == 2:
                    f_re, f_im = -f_re, -f_im
                fwd_ref[w, 0, comp] = dip_ref[w, 0, comp].astype(jnp.float32) - (a_re * f_re - a_im * f_im)
                fwd_ref[w, 1, comp] = dip_ref[w, 1, comp].astype(jnp.float32) - (a_re * f_im + a_im * f_re)
                b_re, b_im = pick(0, 1, which), -pick(1, 1, which)
                if comp == 5:
                    b_re, b_im = -b_re, -b_im
                out_ref[w, 0, comp] = adj_ref[w, 0, comp].astype(jnp.float32) - b_re
                out_ref[w, 1, comp] = adj_ref[w, 1, comp].astype(jnp.float32) - b_im


def vmem(count):
    return [pl.BlockSpec(memory_space=pltpu.VMEM)] * count


def per_device(lattice, material, polarizability, wavenumber, dipoles, adjoint_in):
    n_tgt, n_src = lax.axis_size("tgt"), lax.axis_size("src")
    depth = n_tgt // BANDS
    waves, excite, atoms = dipoles.shape[0], dipoles.shape[3], dipoles.shape[4]
    kinds = polarizability.shape[0]
    width = waves * 24 * excite
    payload, alpha = pl.pallas_call(
        pack_kernel,
        in_specs=vmem(5),
        out_specs=vmem(2),
        out_shape=(
            jax.ShapeDtypeStruct((atoms, width), jnp.bfloat16),
            jax.ShapeDtypeStruct((kinds, waves, atoms), jnp.float32),
        ),
        name="pack",
    )(lattice, material.reshape(1, atoms), jnp.transpose(polarizability, (0, 2, 1)), dipoles, adjoint_in)
    tiles = [payload] + [
        lax.ppermute(payload, AXES, pairs(n_tgt, n_src, k, 0, 0)) for k in range(1, depth)
    ]
    kernels = pl.pallas_call(
        functools.partial(green_kernel, n_tgt=n_tgt, n_src=n_src),
        in_specs=[pl.BlockSpec(memory_space=pltpu.SMEM)],
        out_specs=pl.BlockSpec(memory_space=pltpu.VMEM),
        out_shape=jax.ShapeDtypeStruct((waves, 6, 2 * depth * atoms, 3 * BANDS * atoms), jnp.bfloat16),
        name="green",
    )(wavenumber)
    own, sent = pl.pallas_call(
        field_kernel,
        in_specs=vmem(depth + 1),
        out_specs=vmem(2),
        out_shape=(
            jax.ShapeDtypeStruct((atoms, width), jnp.float32),
            jax.ShapeDtypeStruct((3 * BANDS - 1, atoms, width), jnp.bfloat16),
        ),
        name="fields",
    )(*tiles, kernels)
    got = []
    for index in range(3 * BANDS - 1):
        slot, flip = divmod(index + 1, BANDS)
        got.append(lax.ppermute(sent[index], AXES, pairs(n_tgt, n_src, 0, flip, slot)))
    return pl.pallas_call(
        finish_kernel,
        in_specs=vmem(5 + len(got)),
        out_specs=vmem(2),
        out_shape=(
            jax.ShapeDtypeStruct(dipoles.shape, jnp.float32),
            jax.ShapeDtypeStruct(dipoles.shape, jnp.float32),
        ),
        name="finish",
    )(lattice, alpha, dipoles, adjoint_in, own, *got)


def solution(mesh):
    split = P(None, None, None, None, AXES)
    return jax.shard_map(
        per_device,
        mesh=mesh,
        in_specs=(P(None, AXES), P(AXES), P(), P(), split, split),
        out_specs=(split, split),
        check_vma=False,
    )
```

time: 62.3 us -> 27.9 us (0.45)
  blocking collectives: 32.6 us -> 0 us
  Pallas kernels: 0 us -> 10.9 us
  other arithmetic: 9.25 us -> 0 us
  starting transfers between devices: 2.41 us -> 10.6 us
  matrix products: 7.54 us -> 0 us
  local copies, waits for them, and re-layouts: 5.54 us -> 2.63 us
  between operations: 1.89 us -> 0.67 us
    all_gather x1 -> x0, blocking collectives: 32.6 us -> none  [per_device(): piece = lax.all_gather(widened, 'tgt', axis=1, tiled=True)]
    pallas_call x0 -> x4, Pallas kernels: none -> 10.9 us  [the longest x1 3.9 us: per_device(): pl.pallas_call(functools.partial(green_kernel, n_tgt=n_tgt, n_src=n_src),...]
    ppermute x2 -> x8, starting transfers between devices: 2.41 us -> 10.6 us  [the longest x3 5.64 us: per_device(): lax.ppermute(payload, AXES, pairs(n_tgt, n_src, k, 0, 0))]
    dot_general x48 -> x0, matrix products: 7.42 us -> none  [the longest x24 3.71 us: kernel_products(): jnp.dot(picked, kernel_pair[1], preferred_element_type=jnp.float32)]
    another operation x70 -> x0, other arithmetic: 7.13 us -> none
    slice x8 -> x0, local copies, waits for them, and re-layouts: 1.84 us -> none  [the longest x5 0.78 us: column_fields(): values[wave_index]]
    unnamed x43 -> x16, local copies, waits for them, and re-layouts: 3.13 us -> 1.81 us
    sub x27 -> x0, other arithmetic: 0.96 us -> none  [the longest x1 0.67 us: finish_outputs(): adjoint_out = adjoint_in.astype(jnp.float32) - adjoint_field]
  transfers between devices with their start and end apart: 2 -> 8, of which waited for: 2 -> 3; matrix products, arithmetic and copies ran while one was open for 1% -> 0% of each run, Pallas kernels for 0% -> 14%
where the time goes in v1:
time: 27.9 us; the launch traced here: 27.5 us
  Pallas kernels  10.9 us (39%)
  starting transfers between devices  10.6 us (38%)
  waiting for transfers between devices  2.75 us (10%)
  local copies, waits for them, and re-layouts  2.63 us (9%)
  between operations  0.67 us (2%)
    ppermute x3, starting transfers between devices, per_device(): lax.ppermute(payload, AXES, pairs(n_tgt, n_src, k, 0, 0))  5.64 us
    ppermute x5, starting transfers between devices, per_device(): lax.ppermute(sent[index], AXES, pairs(n_tgt, n_src, 0, flip, slot))  4.91 us
    pallas_call x1, Pallas kernels, per_device(): pl.pallas_call(functools.partial(green_kernel, n_tgt=n_tgt, n_src=n_src),...  3.9 us
    pallas_call x1, Pallas kernels, per_device(): pl.pallas_call(field_kernel, in_specs=vmem(depth + 1), out_specs=vmem(2),...  3.36 us
    ppermute x5, waiting for transfers between devices, per_device(): lax.ppermute(sent[index], AXES, pairs(n_tgt, n_src, 0, flip, slot))  2.29 us
    pallas_call x1, Pallas kernels, per_device(): pl.pallas_call(finish_kernel, in_specs=vmem(5 + len(got)), out_specs=vmem...  1.84 us
    pallas_call x1, Pallas kernels, per_device(): pl.pallas_call(pack_kernel, in_specs=vmem(5), out_specs=vmem(2), out_shap...  1.83 us
    unnamed x16, local copies, waits for them, and re-layouts  1.81 us
  transfers between devices with their start and end apart: 8, of which 3 were waited for; matrix products, arithmetic and copies ran while one was open for 0% of the time, Pallas kernels for 14%

profile of v1, /device:TPU:0, one launch (start us, length us, event | category | flops | bytes accessed | tf_op | source)
XLA Modules:
  0.0 27.5 jit_solution(7397051675951627990)
XLA Ops:
  0.6 1.8 %pack.1 = (bf16[32,384]{1,0:T(8,128)(2,1)}, f32[4,4,32]{2,1,0:T(4,128)}) custom-call(s32[2,32]{1,0:T(2,128)} %refs_0_.1, s32[1,32]{1,0:T(1,128)} %bitcast.13, f32[4,4,16]{2,1,0:T(4,128)} %bitcast.12, bf16[4,2,6,4,32]{4,3,2,1,0:T(4,128)(2,1)} %refs_2_.1, bf16[4,2,6,4,32]{4,3,2,1,0:T(4,128)(2,1)} %refs_3_.1), custom_call_target="tpu_custom_call" | custom-call | tf_op jit(solution)/shard_map/pack/pallas_call | solution.py:242
  2.5 5.1 %collective-permute-start.2 = (bf16[32,384]{1,0:T(8,128)(2,1)}, bf16[32,384]{1,0:T(8,128)(2,1)S(1)}, u32[]{:S(2)}, u32[]{:S(2)}) collective-permute-start(bf16[32,384]{1,0:T(8,128)(2,1)} %get-tuple-element.7.refs_0_), channel_id=1, source_target_pairs={{0,24},{1,25},{2,26},{3,27},{4,28},{5,29},{6,30},{7,31},{8,16},{9,... | collective-permute-start | bytes 73736 | tf_op jit(solution)/shard_map/ppermute | solution.py:253
  7.5 0.0 collective-permute-start.1
  7.5 0.6 %collective-permute-start = (bf16[32,384]{1,0:T(8,128)(2,1)}, bf16[32,384]{1,0:T(8,128)(2,1)S(1)}, u32[]{:S(2)}, u32[]{:S(2)}) collective-permute-start(bf16[32,384]{1,0:T(8,128)(2,1)} %get-tuple-element.7.refs_0_), channel_id=1, source_target_pairs={{0,8},{1,9},{2,10},{3,11},{4,12},{5,13},{6,14},{7,15},{8,0},{9,1},... | collective-permute-start | bytes 73736 | tf_op jit(solution)/shard_map/ppermute | solution.py:253
  8.1 3.9 %green.1.refs_4_ = bf16[4,6,256,192]{3,2,1,0:T(8,128)(2,1)} custom-call(f32[4]{0:T(128)} %wave_ref.1), custom_call_target="tpu_custom_call" | custom-call | tf_op jit(solution)/shard_map/green/pallas_call | solution.py:255
  12.0 0.0 collective-permute-done.2.refs_3_
  12.0 0.0 copy-start
  12.0 0.5 %collective-permute-done.1.refs_2_ = bf16[32,384]{1,0:T(8,128)(2,1)S(1)} collective-permute-done((bf16[32,384]{1,0:T(8,128)(2,1)}, bf16[32,384]{1,0:T(8,128)(2,1)S(1)}, u32[]{:S(2)}, u32[]{:S(2)}) %collective-permute-start.1) | collective-permute-done | bytes 24608 | tf_op jit(solution)/shard_map/ppermute | solution.py:253
  12.5 0.0 copy-start.1
  12.5 0.0 collective-permute-done.refs_1_
  12.5 0.1 copy-done
  12.6 0.5 %copy-done.1 = bf16[32,384]{1,0:T(8,128)(2,1)} copy-done((bf16[32,384]{1,0:T(8,128)(2,1)}, bf16[32,384]{1,0:T(8,128)(2,1)S(1)}, u32[]{:S(2)}) %copy-start.1) | copy-done | bytes 24600
  13.1 0.0 copy-start.2
  13.1 0.6 %copy-done.2 = bf16[32,384]{1,0:T(8,128)(2,1)} copy-done((bf16[32,384]{1,0:T(8,128)(2,1)}, bf16[32,384]{1,0:T(8,128)(2,1)S(1)}, u32[]{:S(2)}) %copy-start.2) | copy-done | bytes 24600
  13.7 3.4 %fields.1 = (f32[32,384]{1,0:T(8,128)}, bf16[5,32,384]{2,1,0:T(8,128)(2,1)}) custom-call(bf16[32,384]{1,0:T(8,128)(2,1)} %get-tuple-element.7.refs_0_, bf16[32,384]{1,0:T(8,128)(2,1)} %copy-done.2, bf16[32,384]{1,0:T(8,128)(2,1)} %copy-done.1, bf16[32,384]{1,0:T(8,128)(2,1)} %copy-done, bf16[4,6,256,192]{3,2,1,0:T(8,128)(2,1)} %green.1.refs_4_), custom_call_target="tpu_custom_call" | custom-call | tf_op jit(solution)/shard_map/fields/pallas_call | solution.py:262
  17.1 0.8 %slice_bitcast_fusion = (bf16[32,384]{1,0:T(8,128)(2,1)S(1)}, bf16[32,384]{1,0:T(8,128)(2,1)S(1)}, bf16[32,384]{1,0:T(8,128)(2,1)S(1)}, bf16[32,384]{1,0:T(8,128)(2,1)S(1)}, bf16[32,384]{1,0:T(8,128)(2,1)S(1)}) fusion(bf16[5,32,384]{2,1,0:T(8,128)(2,1)} %get-tuple-element.9), kind=kLoop, calls=%fused_computation | loop fusion | bytes 245760 | tf_op jit(solution)/shard_map/squeeze | solution.py:275
  17.9 0.9 %collective-permute-start.7 = (bf16[32,384]{1,0:T(8,128)(2,1)S(1)}, bf16[32,384]{1,0:T(8,128)(2,1)S(1)}, u32[]{:S(2)}, u32[]{:S(2)}) collective-permute-start(bf16[32,384]{1,0:T(8,128)(2,1)S(1)} %get-tuple-element.10), channel_id=1, source_target_pairs={{0,7},{1,6},{2,5},{3,4},{4,3},{5,2},{6,1},{7,0},{8,15},{9,14},{10,... | collective-permute-start | bytes 73736 | tf_op jit(solution)/shard_map/ppermute | solution.py:275
  18.8 1.8 %collective-permute-start.6 = (bf16[32,384]{1,0:T(8,128)(2,1)S(1)}, bf16[32,384]{1,0:T(8,128)(2,1)S(1)}, u32[]{:S(2)}, u32[]{:S(2)}) collective-permute-start(bf16[32,384]{1,0:T(8,128)(2,1)S(1)} %get-tuple-element.11), channel_id=1, source_target_pairs={{0,3},{1,2},{2,1},{3,0},{4,7},{5,6},{6,5},{7,4},{8,11},{9,10},{10,... | collective-permute-start | bytes 73736 | tf_op jit(solution)/shard_map/ppermute | solution.py:275
  20.6 0.1 collective-permute-start.5
  20.7 0.5 %collective-permute-start.4 = (bf16[32,384]{1,0:T(8,128)(2,1)S(1)}, bf16[32,384]{1,0:T(8,128)(2,1)S(1)}, u32[]{:S(2)}, u32[]{:S(2)}) collective-permute-start(bf16[32,384]{1,0:T(8,128)(2,1)S(1)} %get-tuple-element.13), channel_id=1, source_target_pairs={{0,1},{1,0},{2,3},{3,2},{4,5},{5,4},{6,7},{7,6},{8,9},{9,8},{10,11... | collective-permute-start | bytes 73736 | tf_op jit(solution)/shard_map/ppermute | solution.py:275
  21.3 1.5 %collective-permute-start.3 = (bf16[32,384]{1,0:T(8,128)(2,1)S(1)}, bf16[32,384]{1,0:T(8,128)(2,1)S(1)}, u32[]{:S(2)}, u32[]{:S(2)}) collective-permute-start(bf16[32,384]{1,0:T(8,128)(2,1)S(1)} %get-tuple-element.14), channel_id=1, source_target_pairs={{0,4},{1,5},{2,6},{3,7},{4,0},{5,1},{6,2},{7,3},{8,12},{9,13},{10,... | collective-permute-start | bytes 73736 | tf_op jit(solution)/shard_map/ppermute | solution.py:275
  22.8 0.0 collective-permute-done.7.refs_9_
  22.8 0.0 copy-start.3
  22.8 0.0 collective-permute-done.6.refs_8_
  22.8 0.0 copy-start.4
  22.8 1.3 %collective-permute-done.5.refs_7_ = bf16[32,384]{1,0:T(8,128)(2,1)S(1)} collective-permute-done((bf16[32,384]{1,0:T(8,128)(2,1)S(1)}, bf16[32,384]{1,0:T(8,128)(2,1)S(1)}, u32[]{:S(2)}, u32[]{:S(2)}) %collective-permute-start.5) | collective-permute-done | bytes 24608 | tf_op jit(solution)/shard_map/ppermute | solution.py:275
  24.1 0.0 copy-start.5
  24.1 0.0 collective-permute-done.4.refs_6_
  24.1 0.0 copy-start.6
  24.1 1.0 %collective-permute-done.3.refs_5_ = bf16[32,384]{1,0:T(8,128)(2,1)S(1)} collective-permute-done((bf16[32,384]{1,0:T(8,128)(2,1)S(1)}, bf16[32,384]{1,0:T(8,128)(2,1)S(1)}, u32[]{:S(2)}, u32[]{:S(2)}) %collective-permute-start.3) | collective-permute-done | bytes 24608 | tf_op jit(solution)/shard_map/ppermute | solution.py:275
  25.1 0.0 copy-start.7
  25.1 0.0 copy-done.3
  25.1 0.0 copy-done.4
  25.1 0.0 copy-done.5
  25.1 0.0 copy-done.6
  25.1 0.6 %copy-done.7 = bf16[32,384]{1,0:T(8,128)(2,1)} copy-done((bf16[32,384]{1,0:T(8,128)(2,1)}, bf16[32,384]{1,0:T(8,128)(2,1)S(1)}, u32[]{:S(2)}) %copy-start.7) | copy-done | bytes 24600
  25.7 1.8 %finish.1 = (f32[4,2,6,4,32]{4,3,2,1,0:T(4,128)}, f32[4,2,6,4,32]{4,3,2,1,0:T(4,128)}) custom-call(s32[2,32]{1,0:T(2,128)} %refs_0_.1, f32[4,4,32]{2,1,0:T(4,128)} %get-tuple-element.6.refs_1_, bf16[4,2,6,4,32]{4,3,2,1,0:T(4,128)(2,1)} %refs_2_.1, bf16[4,2,6,4,32]{4,3,2,1,0:T(4,128)(2,1)} %refs_3_.1, f32[32,384]{1,0:T(8,128)} %get-tuple-element.8.refs_4_, ...), custom_call_target="tpu_custom_call" | custom-call | tf_op jit(solution)/shard_map/finish/pallas_call | solution.py:276
Async XLA Ops:
  2.5 9.5 %collective-permute-start.2 = (bf16[32,384]{1,0:T(8,128)(2,1)}, bf16[32,384]{1,0:T(8,128)(2,1)S(1)}, u32[]{:S(2)}, u32[]{:S(2)}) collective-permute-start(bf16[32,384]{1,0:T(8,128)(2,1)} %get-tuple-element.7.refs_0_), channel_id=1, source_target_pairs={{0,24},{1,25},{2,26},{3,27},{4,28},{5,29},{6,30},{7,31},{8,16},{9,... | collective-permute-start | bytes 73736 | tf_op jit(solution)/shard_map/ppermute | solution.py:253
  7.5 4.9 %collective-permute-start.1 = (bf16[32,384]{1,0:T(8,128)(2,1)}, bf16[32,384]{1,0:T(8,128)(2,1)S(1)}, u32[]{:S(2)}, u32[]{:S(2)}) collective-permute-start(bf16[32,384]{1,0:T(8,128)(2,1)} %get-tuple-element.7.refs_0_), channel_id=1, source_target_pairs={{0,16},{1,17},{2,18},{3,19},{4,20},{5,21},{6,22},{7,23},{8,24},{9,... | collective-permute-start | bytes 73736 | tf_op jit(solution)/shard_map/ppermute | solution.py:253
  7.5 4.9 %collective-permute-start = (bf16[32,384]{1,0:T(8,128)(2,1)}, bf16[32,384]{1,0:T(8,128)(2,1)S(1)}, u32[]{:S(2)}, u32[]{:S(2)}) collective-permute-start(bf16[32,384]{1,0:T(8,128)(2,1)} %get-tuple-element.7.refs_0_), channel_id=1, source_target_pairs={{0,8},{1,9},{2,10},{3,11},{4,12},{5,13},{6,14},{7,15},{8,0},{9,1},... | collective-permute-start | bytes 73736 | tf_op jit(solution)/shard_map/ppermute | solution.py:253
  12.0 0.6 %copy-start = (bf16[32,384]{1,0:T(8,128)(2,1)}, bf16[32,384]{1,0:T(8,128)(2,1)S(1)}, u32[]{:S(2)}) copy-start(bf16[32,384]{1,0:T(8,128)(2,1)S(1)} %collective-permute-done.2.refs_3_) | copy-start | bytes 73732
  12.5 0.6 %copy-start.1 = (bf16[32,384]{1,0:T(8,128)(2,1)}, bf16[32,384]{1,0:T(8,128)(2,1)S(1)}, u32[]{:S(2)}) copy-start(bf16[32,384]{1,0:T(8,128)(2,1)S(1)} %collective-permute-done.1.refs_2_) | copy-start | bytes 73732
  13.1 0.6 %copy-start.2 = (bf16[32,384]{1,0:T(8,128)(2,1)}, bf16[32,384]{1,0:T(8,128)(2,1)S(1)}, u32[]{:S(2)}) copy-start(bf16[32,384]{1,0:T(8,128)(2,1)S(1)} %collective-permute-done.refs_1_) | copy-start | bytes 73732
  17.9 4.9 %collective-permute-start.7 = (bf16[32,384]{1,0:T(8,128)(2,1)S(1)}, bf16[32,384]{1,0:T(8,128)(2,1)S(1)}, u32[]{:S(2)}, u32[]{:S(2)}) collective-permute-start(bf16[32,384]{1,0:T(8,128)(2,1)S(1)} %get-tuple-element.10), channel_id=1, source_target_pairs={{0,7},{1,6},{2,5},{3,4},{4,3},{5,2},{6,1},{7,0},{8,15},{9,14},{10,... | collective-permute-start | bytes 73736 | tf_op jit(solution)/shard_map/ppermute | solution.py:275
  18.8 4.0 %collective-permute-start.6 = (bf16[32,384]{1,0:T(8,128)(2,1)S(1)}, bf16[32,384]{1,0:T(8,128)(2,1)S(1)}, u32[]{:S(2)}, u32[]{:S(2)}) collective-permute-start(bf16[32,384]{1,0:T(8,128)(2,1)S(1)} %get-tuple-element.11), channel_id=1, source_target_pairs={{0,3},{1,2},{2,1},{3,0},{4,7},{5,6},{6,5},{7,4},{8,11},{9,10},{10,... | collective-permute-start | bytes 73736 | tf_op jit(solution)/shard_map/ppermute | solution.py:275
  20.6 3.5 %collective-permute-start.5 = (bf16[32,384]{1,0:T(8,128)(2,1)S(1)}, bf16[32,384]{1,0:T(8,128)(2,1)S(1)}, u32[]{:S(2)}, u32[]{:S(2)}) collective-permute-start(bf16[32,384]{1,0:T(8,128)(2,1)S(1)} %get-tuple-element.12), channel_id=1, source_target_pairs={{0,5},{1,4},{2,7},{3,6},{4,1},{5,0},{6,3},{7,2},{8,13},{9,12},{10,... | collective-permute-start | bytes 73736 | tf_op jit(solution)/shard_map/ppermute | solution.py:275
  20.7 3.4 %collective-permute-start.4 = (bf16[32,384]{1,0:T(8,128)(2,1)S(1)}, bf16[32,384]{1,0:T(8,128)(2,1)S(1)}, u32[]{:S(2)}, u32[]{:S(2)}) collective-permute-start(bf16[32,384]{1,0:T(8,128)(2,1)S(1)} %get-tuple-element.13), channel_id=1, source_target_pairs={{0,1},{1,0},{2,3},{3,2},{4,5},{5,4},{6,7},{7,6},{8,9},{9,8},{10,11... | collective-permute-start | bytes 73736 | tf_op jit(solution)/shard_map/ppermute | solution.py:275
  21.3 3.8 %collective-permute-start.3 = (bf16[32,384]{1,0:T(8,128)(2,1)S(1)}, bf16[32,384]{1,0:T(8,128)(2,1)S(1)}, u32[]{:S(2)}, u32[]{:S(2)}) collective-permute-start(bf16[32,384]{1,0:T(8,128)(2,1)S(1)} %get-tuple-element.14), channel_id=1, source_target_pairs={{0,4},{1,5},{2,6},{3,7},{4,0},{5,1},{6,2},{7,3},{8,12},{9,13},{10,... | collective-permute-start | bytes 73736 | tf_op jit(solution)/shard_map/ppermute | solution.py:275
  22.8 2.3 %copy-start.3 = (bf16[32,384]{1,0:T(8,128)(2,1)}, bf16[32,384]{1,0:T(8,128)(2,1)S(1)}, u32[]{:S(2)}) copy-start(bf16[32,384]{1,0:T(8,128)(2,1)S(1)} %collective-permute-done.7.refs_9_) | copy-start | bytes 73732
  22.8 2.3 %copy-start.4 = (bf16[32,384]{1,0:T(8,128)(2,1)}, bf16[32,384]{1,0:T(8,128)(2,1)S(1)}, u32[]{:S(2)}) copy-start(bf16[32,384]{1,0:T(8,128)(2,1)S(1)} %collective-permute-done.6.refs_8_) | copy-start | bytes 73732
  24.1 1.0 %copy-start.5 = (bf16[32,384]{1,0:T(8,128)(2,1)}, bf16[32,384]{1,0:T(8,128)(2,1)S(1)}, u32[]{:S(2)}) copy-start(bf16[32,384]{1,0:T(8,128)(2,1)S(1)} %collective-permute-done.5.refs_7_) | copy-start | bytes 73732
  24.1 1.0 %copy-start.6 = (bf16[32,384]{1,0:T(8,128)(2,1)}, bf16[32,384]{1,0:T(8,128)(2,1)S(1)}, u32[]{:S(2)}) copy-start(bf16[32,384]{1,0:T(8,128)(2,1)S(1)} %collective-permute-done.4.refs_6_) | copy-start | bytes 73732
  25.1 0.6 %copy-start.7 = (bf16[32,384]{1,0:T(8,128)(2,1)}, bf16[32,384]{1,0:T(8,128)(2,1)S(1)}, u32[]{:S(2)}) copy-start(bf16[32,384]{1,0:T(8,128)(2,1)S(1)} %collective-permute-done.3.refs_5_) | copy-start | bytes 73732

commit v2 on v1

--- a/solution.py
+++ b/solution.py
@@ -45,9 +45,19 @@
     return (lattice[0:1] % TILE_X) * TILE_Y + lattice[1:2] % TILE_Y
 
 
-def pack_kernel(lattice_ref, material_ref, pol_ref, dip_ref, adj_ref, payload_ref, alpha_ref):
+def pack_kernel(*refs):
+    sources, (payload_ref, alpha_ref, waves_ref, place_ref), scratch = refs[:6], refs[6:10], refs[10:]
+    copies = [pltpu.make_async_copy(source, there, scratch[-1].at[i]) for i, (source, there) in enumerate(zip(sources, scratch))]
+    for copy in copies:
+        copy.start()
+    for copy in copies:
+        copy.wait()
+    lattice_ref, material_ref, pol_ref, wave_ref, dip_ref, adj_ref = scratch[:6]
     waves, _, _, excite, atoms = dip_ref.shape
     types = pol_ref.shape[2]
+    for w in range(waves):
+        waves_ref[w : w + 1] = jnp.broadcast_to(wave_ref[0:1, w : w + 1], (1, waves_ref.shape[1]))
+    place_ref[...] = jnp.broadcast_to(lattice_ref[:, 0:1], place_ref.shape)
     kinds = lax.broadcasted_iota(jnp.int32, (types, atoms), 0)
     onehot = jnp.where(kinds == material_ref[...], 1.0, 0.0).astype(jnp.float32)
     alpha = []
@@ -103,12 +113,12 @@
     return sin, cos
 
 
-def green_kernel(wave_ref, out_ref, *, n_tgt, n_src):
+def green_kernel(wave_ref, place_ref, out_ref, *, n_tgt, n_src):
     waves, _, double, targets = out_ref.shape
     sources = double // 2
     depth = n_tgt // BANDS
-    band = lax.axis_index("tgt")
-    column = lax.axis_index("src")
+    band = place_ref[0:1] // TILE_X
+    column = place_ref[1:2] // TILE_Y
     z, y = band // BANDS, band % BANDS
     period = n_src * TILE_Y
     if n_src % 2:
@@ -137,7 +147,7 @@
         xx, yy, xy = ux * ux, uy * uy, ux * uy
         ux = -ux
         for w in range(waves):
-            wave = wave_ref[w]
+            wave = wave_ref[w : w + 1]
             sin, cos = sin_cos(wave * radius)
             inv = inverse * (1.0 / wave)
             g_re = cos * inv
@@ -161,7 +171,7 @@
 
 
 def field_kernel(*refs):
-    *tile_refs, kernels_ref, own_ref, sent_ref = refs
+    *tile_refs, kernels_ref, own_ref, core_ref, flip_ref, side_ref, cross_ref = refs
     waves = kernels_ref.shape[0]
     gathered = jnp.concatenate([ref[...].astype(jnp.float32) for ref in tile_refs], axis=0)
     rows = gathered.T.astype(jnp.bfloat16)
@@ -186,16 +196,20 @@
                 total[c_out] = piece if total[c_out] is None else total[c_out] + piece
         fields += total
     turned = jnp.concatenate(fields, axis=0).T
-    own_ref[...] = turned[:ATOMS]
-    for index in range(sent_ref.shape[0]):
-        sent_ref[index] = turned[(index + 1) * ATOMS : (index + 2) * ATOMS].astype(jnp.bfloat16)
+    piece = lambda slot, flip: turned[(slot * BANDS + flip) * ATOMS :][:ATOMS]
+    own_ref[...] = piece(0, 0)
+    core_ref[...] = piece(1, 0)
+    flip_ref[0] = piece(0, 1).astype(jnp.bfloat16)
+    flip_ref[1] = piece(1, 1).astype(jnp.bfloat16)
+    side_ref[...] = piece(2, 0).astype(jnp.bfloat16)
+    cross_ref[...] = piece(2, 1).astype(jnp.bfloat16)
 
 
 def finish_kernel(*refs):
     lattice_ref, alpha_ref, dip_ref, adj_ref, own_ref, *rest = refs
-    *got_refs, fwd_ref, out_ref = rest
+    flip_ref, *got_refs, fwd_ref, out_ref = rest
     waves, _, _, excite, atoms = dip_ref.shape
-    field = own_ref[...]
+    field = own_ref[...] + flip_ref[0].astype(jnp.float32)
     for ref in got_refs:
         field = field + ref[...].astype(jnp.float32)
     high = field.astype(jnp.bfloat16)
@@ -239,40 +253,55 @@
     waves, excite, atoms = dipoles.shape[0], dipoles.shape[3], dipoles.shape[4]
     kinds = polarizability.shape[0]
     width = waves * 24 * excite
-    payload, alpha = pl.pallas_call(
+    arguments = (
+        lattice,
+        material.reshape(1, atoms),
+        jnp.transpose(polarizability, (0, 2, 1)),
+        wavenumber.reshape(1, waves),
+        dipoles,
+        adjoint_in,
+    )
+    targets = 3 * BANDS * atoms
+    payload, alpha, wave_rows, place = pl.pallas_call(
         pack_kernel,
-        in_specs=vmem(5),
-        out_specs=vmem(2),
+        in_specs=[pl.BlockSpec(memory_space=pltpu.HBM)] * len(arguments),
+        out_specs=vmem(4),
         out_shape=(
             jax.ShapeDtypeStruct((atoms, width), jnp.bfloat16),
             jax.ShapeDtypeStruct((kinds, waves, atoms), jnp.float32),
+            jax.ShapeDtypeStruct((waves, targets), jnp.float32),
+            jax.ShapeDtypeStruct((2, targets), jnp.int32),
         ),
+        scratch_shapes=[pltpu.VMEM(x.shape, x.dtype) for x in arguments]
+        + [pltpu.SemaphoreType.DMA((len(arguments),))],
+        compiler_params=pltpu.CompilerParams(vmem_limit_bytes=4 << 20),
         name="pack",
-    )(lattice, material.reshape(1, atoms), jnp.transpose(polarizability, (0, 2, 1)), dipoles, adjoint_in)
-    tiles = [payload] + [
-        lax.ppermute(payload, AXES, pairs(n_tgt, n_src, k, 0, 0)) for k in range(1, depth)
-    ]
+    )(*(pltpu.with_memory_space_constraint(x, pltpu.HBM) for x in arguments))
+    send = lambda x, shift, flip, slot: lax.ppermute(x, AXES, pairs(n_tgt, n_src, shift, flip, slot))
+    tiles = [payload] + [send(payload, k, 0, 0) for k in range(1, depth)]
     kernels = pl.pallas_call(
         functools.partial(green_kernel, n_tgt=n_tgt, n_src=n_src),
-        in_specs=[pl.BlockSpec(memory_space=pltpu.SMEM)],
+        in_specs=vmem(2),
         out_specs=pl.BlockSpec(memory_space=pltpu.VMEM),
-        out_shape=jax.ShapeDtypeStruct((waves, 6, 2 * depth * atoms, 3 * BANDS * atoms), jnp.bfloat16),
+        out_shape=jax.ShapeDtypeStruct((waves, 6, 2 * depth * atoms, targets), jnp.bfloat16),
+        compiler_params=pltpu.CompilerParams(vmem_limit_bytes=12 << 20),
         name="green",
-    )(wavenumber)
-    own, sent = pl.pallas_call(
+    )(wave_rows, place)
+    tile = jax.ShapeDtypeStruct((atoms, width), jnp.bfloat16)
+    wide = jax.ShapeDtypeStruct((atoms, width), jnp.float32)
+    own, core, flip, side, cross = pl.pallas_call(
         field_kernel,
         in_specs=vmem(depth + 1),
-        out_specs=vmem(2),
-        out_shape=(
-            jax.ShapeDtypeStruct((atoms, width), jnp.float32),
-            jax.ShapeDtypeStruct((3 * BANDS - 1, atoms, width), jnp.bfloat16),
-        ),
+        out_specs=vmem(5),
+        out_shape=(wide, wide, jax.ShapeDtypeStruct((2, atoms, width), jnp.bfloat16), tile, tile),
+        compiler_params=pltpu.CompilerParams(vmem_limit_bytes=12 << 20),
         name="fields",
     )(*tiles, kernels)
-    got = []
-    for index in range(3 * BANDS - 1):
-        slot, flip = divmod(index + 1, BANDS)
-        got.append(lax.ppermute(sent[index], AXES, pairs(n_tgt, n_src, 0, flip, slot)))
+    cross = send(cross, 0, 1, 2)
+    side = send(side, 0, 0, 2)
+    flip = send(flip, 0, 1, 0)
+    core = send((core + flip[1].astype(jnp.float32)).astype(jnp.bfloat16), 0, 0, 1)
+    got = (flip, side, cross, core)
     return pl.pallas_call(
         finish_kernel,
         in_specs=vmem(5 + len(got)),
@@ -281,6 +310,7 @@
             jax.ShapeDtypeStruct(dipoles.shape, jnp.float32),
             jax.ShapeDtypeStruct(dipoles.shape, jnp.float32),
         ),
+        compiler_params=pltpu.CompilerParams(vmem_limit_bytes=8 << 20),
         name="finish",
     )(lattice, alpha, dipoles, adjoint_in, own, *got)
 

time: 27.9 us -> 20.5 us (0.73)
  the two profiles are of different devices: /device:TPU:0 before, /device:TPU:1 now
where the time goes in v2:
time: 20.5 us; the launch traced here: 20.3 us
  starting transfers between devices  10.9 us (53%)
  Pallas kernels  4.44 us (22%)
  waiting for transfers between devices  4.31 us (21%)
  between operations  0.68 us (3%)
    ppermute x7, starting transfers between devices, per_device(): lax.ppermute(x, AXES, pairs(n_tgt, n_src, shift, flip, slot))  10.9 us
    ppermute x7, waiting for transfers between devices, per_device(): lax.ppermute(x, AXES, pairs(n_tgt, n_src, shift, flip, slot))  4.31 us
    pallas_call x1, Pallas kernels, per_device(): pl.pallas_call(functools.partial(green_kernel, n_tgt=n_tgt, n_src=n_src),...  1.49 us
    pallas_call x1, Pallas kernels, per_device(): pl.pallas_call(pack_kernel, in_specs=[pl.BlockSpec(memory_space=pltpu.HBM...  1.29 us
    pallas_call x1, Pallas kernels, per_device(): pl.pallas_call(finish_kernel, in_specs=vmem(5 + len(got)), out_specs=vmem...  0.93 us
    pallas_call x1, Pallas kernels, per_device(): pl.pallas_call(field_kernel, in_specs=vmem(depth + 1), out_specs=vmem(5),...  0.74 us
  transfers between devices with their start and end apart: 7, of which 3 were waited for; matrix products, arithmetic and copies ran while one was open for 0% of the time, Pallas kernels for 7%

profile of v2, /device:TPU:1, one launch (start us, length us, event | category | flops | bytes accessed | tf_op | source)
XLA Modules:
  0.0 20.3 jit_solution(16442974371649382215)
XLA Ops:
  0.6 1.3 %pack.1 = (bf16[32,384]{1,0:T(8,128)(2,1)S(1)}, f32[4,4,32]{2,1,0:T(4,128)S(1)}, f32[4,192]{1,0:T(4,128)S(1)}, s32[2,192]{1,0:T(2,128)S(1)}) custom-call(s32[2,32]{1,0:T(2,128)} %refs_0_.3, s32[1,32]{1,0:T(1,128)} %bitcast.9, f32[4,4,16]{2,1,0:T(4,128)} %bitcast.8, f32[1,4]{1,0:T(1,128)} %bitcast.10, bf16[4,2,6,4,32]{4,3,2,1,0:T(4,128)(2,1)} %refs_2_.1, ...), custom_call_target="tpu_custom_call" | custom-call | tf_op jit(solution)/shard_map/pack/pallas_call | solution.py:265
  1.9 4.2 %collective-permute-start.2 = (bf16[32,384]{1,0:T(8,128)(2,1)S(1)}, bf16[32,384]{1,0:T(8,128)(2,1)S(1)}, u32[]{:S(2)}, u32[]{:S(2)}) collective-permute-start(bf16[32,384]{1,0:T(8,128)(2,1)S(1)} %get-tuple-element.12.refs_0_), channel_id=1, source_target_pairs={{0,24},{1,25},{2,26},{3,27},{4,28},{5,29},{6,30},{7,31},{8,16},{9,... | collective-permute-start | bytes 73736 | tf_op jit(solution)/shard_map/ppermute | solution.py:280
  6.1 0.0 collective-permute-start.1
  6.1 0.4 %collective-permute-start = (bf16[32,384]{1,0:T(8,128)(2,1)S(1)}, bf16[32,384]{1,0:T(8,128)(2,1)S(1)}, u32[]{:S(2)}, u32[]{:S(2)}) collective-permute-start(bf16[32,384]{1,0:T(8,128)(2,1)S(1)} %get-tuple-element.12.refs_0_), channel_id=1, source_target_pairs={{0,8},{1,9},{2,10},{3,11},{4,12},{5,13},{6,14},{7,15},{8,0},{9,1},... | collective-permute-start | bytes 73736 | tf_op jit(solution)/shard_map/ppermute | solution.py:280
  6.5 0.0 copy-start
  6.5 0.0 copy-start.1
  6.5 0.0 copy-start.2
  6.5 1.5 %green.1.refs_4_ = bf16[4,6,256,192]{3,2,1,0:T(8,128)(2,1)S(1)} custom-call(f32[4,192]{1,0:T(4,128)S(1)} %get-tuple-element.13.wave_ref, s32[2,192]{1,0:T(2,128)S(1)} %get-tuple-element.14.place_ref), custom_call_target="tpu_custom_call" | custom-call | tf_op jit(solution)/shard_map/green/pallas_call | solution.py:282
  8.0 0.0 collective-permute-done.2.refs_3_
  8.0 1.7 %collective-permute-done.1.refs_2_ = bf16[32,384]{1,0:T(8,128)(2,1)S(1)} collective-permute-done((bf16[32,384]{1,0:T(8,128)(2,1)S(1)}, bf16[32,384]{1,0:T(8,128)(2,1)S(1)}, u32[]{:S(2)}, u32[]{:S(2)}) %collective-permute-start.1) | collective-permute-done | bytes 24608 | tf_op jit(solution)/shard_map/ppermute | solution.py:280
  9.7 0.0 collective-permute-done.refs_1_
  9.7 0.7 %fields.1 = (f32[32,384]{1,0:T(8,128)S(1)}, f32[32,384]{1,0:T(8,128)S(1)}, bf16[2,32,384]{2,1,0:T(8,128)(2,1)S(1)}, bf16[32,384]{1,0:T(8,128)(2,1)S(1)}, bf16[32,384]{1,0:T(8,128)(2,1)S(1)}) custom-call(bf16[32,384]{1,0:T(8,128)(2,1)S(1)} %get-tuple-element.12.refs_0_, bf16[32,384]{1,0:T(8,128)(2,1)S(1)} %collective-permute-done.refs_1_, ...), custom_call_target="tpu_custom_call" | custom-call | tf_op jit(solution)/shard_map/fields/pallas_call | solution.py:292
  10.4 1.3 %collective-permute-start.3 = (bf16[2,32,384]{2,1,0:T(8,128)(2,1)S(1)}, bf16[2,32,384]{2,1,0:T(8,128)(2,1)S(1)}, u32[]{:S(2)}, u32[]{:S(2)}) collective-permute-start(bf16[2,32,384]{2,1,0:T(8,128)(2,1)S(1)} %get-tuple-element.16), channel_id=1, source_target_pairs={{0,4},{1,5},{2,6},{3,7},{4,0},{5,1},{6,2},{7,3},{8,12},{9,13},{10,... | collective-permute-start | bytes 147464 | tf_op jit(solution)/shard_map/ppermute | solution.py:280
  11.8 3.5 %collective-permute-start.4 = (bf16[32,384]{1,0:T(8,128)(2,1)S(1)}, bf16[32,384]{1,0:T(8,128)(2,1)S(1)}, u32[]{:S(2)}, u32[]{:S(2)}) collective-permute-start(bf16[32,384]{1,0:T(8,128)(2,1)S(1)} %get-tuple-element.17), channel_id=1, source_target_pairs={{0,3},{1,2},{2,1},{3,0},{4,7},{5,6},{6,5},{7,4},{8,11},{9,10},{10,... | collective-permute-start | bytes 73736 | tf_op jit(solution)/shard_map/ppermute | solution.py:280
  15.2 0.0 collective-permute-start.5
  15.2 0.0 collective-permute-done.3.refs_5_
  15.3 1.5 %collective-permute-start.6 = (bf16[32,384]{1,0:T(8,128)(2,1)S(1)}, bf16[32,384]{1,0:T(8,128)(2,1)S(1)}, u32[]{:S(2)}, u32[]{:S(2)}) collective-permute-start(bf16[32,384]{1,0:T(8,128)(2,1)S(1)} %fusion), channel_id=1, source_target_pairs={{0,1},{1,0},{2,3},{3,2},{4,5},{5,4},{6,7},{7,6},{8,9},{9,8},{10,11... | collective-permute-start | bytes 73736 | tf_op jit(solution)/shard_map/ppermute | solution.py:280
  16.8 0.4 %collective-permute-done.4.refs_6_ = bf16[32,384]{1,0:T(8,128)(2,1)S(1)} collective-permute-done((bf16[32,384]{1,0:T(8,128)(2,1)S(1)}, bf16[32,384]{1,0:T(8,128)(2,1)S(1)}, u32[]{:S(2)}, u32[]{:S(2)}) %collective-permute-start.4) | collective-permute-done | bytes 24608 | tf_op jit(solution)/shard_map/ppermute | solution.py:280
  17.2 2.2 %collective-permute-done.5.refs_7_ = bf16[32,384]{1,0:T(8,128)(2,1)S(1)} collective-permute-done((bf16[32,384]{1,0:T(8,128)(2,1)S(1)}, bf16[32,384]{1,0:T(8,128)(2,1)S(1)}, u32[]{:S(2)}, u32[]{:S(2)}) %collective-permute-start.5) | collective-permute-done | bytes 24608 | tf_op jit(solution)/shard_map/ppermute | solution.py:280
  19.4 0.0 collective-permute-done.6.refs_8_
  19.4 0.0 copy-done
  19.4 0.0 copy-done.1
  19.4 0.0 copy-done.2
  19.4 0.9 %finish.1 = (f32[4,2,6,4,32]{4,3,2,1,0:T(4,128)}, f32[4,2,6,4,32]{4,3,2,1,0:T(4,128)}) custom-call(s32[2,32]{1,0:T(2,128)S(1)} %copy-done.2, f32[4,4,32]{2,1,0:T(4,128)S(1)} %get-tuple-element.11.refs_1_, bf16[4,2,6,4,32]{4,3,2,1,0:T(4,128)(2,1)S(1)} %copy-done, bf16[4,2,6,4,32]{4,3,2,1,0:T(4,128)(2,1)S(1)} %copy-done.1, ...), custom_call_target="tpu_custom_call" | custom-call | tf_op jit(solution)/shard_map/finish/pallas_call | solution.py:305
  (1 shorter events, 0.0 us)
Async XLA Ops:
  1.9 6.1 %collective-permute-start.2 = (bf16[32,384]{1,0:T(8,128)(2,1)S(1)}, bf16[32,384]{1,0:T(8,128)(2,1)S(1)}, u32[]{:S(2)}, u32[]{:S(2)}) collective-permute-start(bf16[32,384]{1,0:T(8,128)(2,1)S(1)} %get-tuple-element.12.refs_0_), channel_id=1, source_target_pairs={{0,24},{1,25},{2,26},{3,27},{4,28},{5,29},{6,30},{7,31},{8,16},{9,... | collective-permute-start | bytes 73736 | tf_op jit(solution)/shard_map/ppermute | solution.py:280
  6.1 3.6 %collective-permute-start.1 = (bf16[32,384]{1,0:T(8,128)(2,1)S(1)}, bf16[32,384]{1,0:T(8,128)(2,1)S(1)}, u32[]{:S(2)}, u32[]{:S(2)}) collective-permute-start(bf16[32,384]{1,0:T(8,128)(2,1)S(1)} %get-tuple-element.12.refs_0_), channel_id=1, source_target_pairs={{0,16},{1,17},{2,18},{3,19},{4,20},{5,21},{6,22},{7,23},{8,24},{9,... | collective-permute-start | bytes 73736 | tf_op jit(solution)/shard_map/ppermute | solution.py:280
  6.1 3.6 %collective-permute-start = (bf16[32,384]{1,0:T(8,128)(2,1)S(1)}, bf16[32,384]{1,0:T(8,128)(2,1)S(1)}, u32[]{:S(2)}, u32[]{:S(2)}) collective-permute-start(bf16[32,384]{1,0:T(8,128)(2,1)S(1)} %get-tuple-element.12.refs_0_), channel_id=1, source_target_pairs={{0,8},{1,9},{2,10},{3,11},{4,12},{5,13},{6,14},{7,15},{8,0},{9,1},... | collective-permute-start | bytes 73736 | tf_op jit(solution)/shard_map/ppermute | solution.py:280
  6.5 12.9 %copy-start = (bf16[4,2,6,4,32]{4,3,2,1,0:T(4,128)(2,1)S(1)}, bf16[4,2,6,4,32]{4,3,2,1,0:T(4,128)(2,1)}, u32[]{:S(2)}) copy-start(bf16[4,2,6,4,32]{4,3,2,1,0:T(4,128)(2,1)} %refs_2_.1) | copy-start | bytes 36868
  6.5 12.9 %copy-start.1 = (bf16[4,2,6,4,32]{4,3,2,1,0:T(4,128)(2,1)S(1)}, bf16[4,2,6,4,32]{4,3,2,1,0:T(4,128)(2,1)}, u32[]{:S(2)}) copy-start(bf16[4,2,6,4,32]{4,3,2,1,0:T(4,128)(2,1)} %refs_3_.1) | copy-start | bytes 36868
  6.5 12.9 %copy-start.2 = (s32[2,32]{1,0:T(2,128)S(1)}, s32[2,32]{1,0:T(2,128)}, u32[]{:S(2)}) copy-start(s32[2,32]{1,0:T(2,128)} %refs_0_.3) | copy-start | bytes 772
  10.4 4.8 %collective-permute-start.3 = (bf16[2,32,384]{2,1,0:T(8,128)(2,1)S(1)}, bf16[2,32,384]{2,1,0:T(8,128)(2,1)S(1)}, u32[]{:S(2)}, u32[]{:S(2)}) collective-permute-start(bf16[2,32,384]{2,1,0:T(8,128)(2,1)S(1)} %get-tuple-element.16), channel_id=1, source_target_pairs={{0,4},{1,5},{2,6},{3,7},{4,0},{5,1},{6,2},{7,3},{8,12},{9,13},{10,... | collective-permute-start | bytes 147464 | tf_op jit(solution)/shard_map/ppermute | solution.py:280
  11.8 5.5 %collective-permute-start.4 = (bf16[32,384]{1,0:T(8,128)(2,1)S(1)}, bf16[32,384]{1,0:T(8,128)(2,1)S(1)}, u32[]{:S(2)}, u32[]{:S(2)}) collective-permute-start(bf16[32,384]{1,0:T(8,128)(2,1)S(1)} %get-tuple-element.17), channel_id=1, source_target_pairs={{0,3},{1,2},{2,1},{3,0},{4,7},{5,6},{6,5},{7,4},{8,11},{9,10},{10,... | collective-permute-start | bytes 73736 | tf_op jit(solution)/shard_map/ppermute | solution.py:280
  15.2 4.2 %collective-permute-start.5 = (bf16[32,384]{1,0:T(8,128)(2,1)S(1)}, bf16[32,384]{1,0:T(8,128)(2,1)S(1)}, u32[]{:S(2)}, u32[]{:S(2)}) collective-permute-start(bf16[32,384]{1,0:T(8,128)(2,1)S(1)} %get-tuple-element.18), channel_id=1, source_target_pairs={{0,7},{1,6},{2,5},{3,4},{4,3},{5,2},{6,1},{7,0},{8,15},{9,14},{10,... | collective-permute-start | bytes 73736 | tf_op jit(solution)/shard_map/ppermute | solution.py:280
  15.3 4.1 %collective-permute-start.6 = (bf16[32,384]{1,0:T(8,128)(2,1)S(1)}, bf16[32,384]{1,0:T(8,128)(2,1)S(1)}, u32[]{:S(2)}, u32[]{:S(2)}) collective-permute-start(bf16[32,384]{1,0:T(8,128)(2,1)S(1)} %fusion), channel_id=1, source_target_pairs={{0,1},{1,0},{2,3},{3,2},{4,5},{5,4},{6,7},{7,6},{8,9},{9,8},{10,11... | collective-permute-start | bytes 73736 | tf_op jit(solution)/shard_map/ppermute | solution.py:280

commit v3 on v2

--- a/solution.py
+++ b/solution.py
@@ -207,7 +207,8 @@
 
 def finish_kernel(*refs):
     lattice_ref, alpha_ref, dip_ref, adj_ref, own_ref, *rest = refs
-    flip_ref, *got_refs, fwd_ref, out_ref = rest
+    *got_refs, fwd_ref, out_ref = rest
+    flip_ref = got_refs.pop(2)
     waves, _, _, excite, atoms = dip_ref.shape
     field = own_ref[...] + flip_ref[0].astype(jnp.float32)
     for ref in got_refs:
@@ -301,7 +302,7 @@
     side = send(side, 0, 0, 2)
     flip = send(flip, 0, 1, 0)
     core = send((core + flip[1].astype(jnp.float32)).astype(jnp.bfloat16), 0, 0, 1)
-    got = (flip, side, cross, core)
+    got = (cross, side, flip, core)
     return pl.pallas_call(
         finish_kernel,
         in_specs=vmem(5 + len(got)),

time: 20.5 us -> 19.6 us (0.956)
  the two profiles are of different devices: /device:TPU:1 before, /device:TPU:0 now
where the time goes in v3:
time: 19.6 us; the launch traced here: 19.2 us
  starting transfers between devices  9.13 us (47%)
  waiting for transfers between devices  4.94 us (25%)
  Pallas kernels  4.45 us (23%)
  between operations  0.69 us (4%)
    ppermute x7, starting transfers between devices, per_device(): lax.ppermute(x, AXES, pairs(n_tgt, n_src, shift, flip, slot))  9.13 us
    ppermute x7, waiting for transfers between devices, per_device(): lax.ppermute(x, AXES, pairs(n_tgt, n_src, shift, flip, slot))  4.94 us
    pallas_call x1, Pallas kernels, per_device(): pl.pallas_call(functools.partial(green_kernel, n_tgt=n_tgt, n_src=n_src),...  1.49 us
    pallas_call x1, Pallas kernels, per_device(): pl.pallas_call(pack_kernel, in_specs=[pl.BlockSpec(memory_space=pltpu.HBM...  1.29 us
    pallas_call x1, Pallas kernels, per_device(): pl.pallas_call(finish_kernel, in_specs=vmem(5 + len(got)), out_specs=vmem...  0.93 us
    pallas_call x1, Pallas kernels, per_device(): pl.pallas_call(field_kernel, in_specs=vmem(depth + 1), out_specs=vmem(5),...  0.74 us
  transfers between devices with their start and end apart: 7, of which 3 were waited for; matrix products, arithmetic and copies ran while one was open for 0% of the time, Pallas kernels for 8%

profile of v3, /device:TPU:0, one launch (start us, length us, event | category | flops | bytes accessed | tf_op | source)
XLA Modules:
  0.0 19.2 jit_solution(13366993787750077634)
XLA Ops:
  0.6 1.3 %pack.1 = (bf16[32,384]{1,0:T(8,128)(2,1)S(1)}, f32[4,4,32]{2,1,0:T(4,128)S(1)}, f32[4,192]{1,0:T(4,128)S(1)}, s32[2,192]{1,0:T(2,128)S(1)}) custom-call(s32[2,32]{1,0:T(2,128)} %refs_0_.3, s32[1,32]{1,0:T(1,128)} %bitcast.9, f32[4,4,16]{2,1,0:T(4,128)} %bitcast.8, f32[1,4]{1,0:T(1,128)} %bitcast.10, bf16[4,2,6,4,32]{4,3,2,1,0:T(4,128)(2,1)} %refs_2_.1, ...), custom_call_target="tpu_custom_call" | custom-call | tf_op jit(solution)/shard_map/pack/pallas_call | solution.py:266
  1.9 5.1 %collective-permute-start.2 = (bf16[32,384]{1,0:T(8,128)(2,1)S(1)}, bf16[32,384]{1,0:T(8,128)(2,1)S(1)}, u32[]{:S(2)}, u32[]{:S(2)}) collective-permute-start(bf16[32,384]{1,0:T(8,128)(2,1)S(1)} %get-tuple-element.12.refs_0_), channel_id=1, source_target_pairs={{0,24},{1,25},{2,26},{3,27},{4,28},{5,29},{6,30},{7,31},{8,16},{9,... | collective-permute-start | bytes 73736 | tf_op jit(solution)/shard_map/ppermute | solution.py:281
  7.1 0.0 collective-permute-start.1
  7.1 0.6 %collective-permute-start = (bf16[32,384]{1,0:T(8,128)(2,1)S(1)}, bf16[32,384]{1,0:T(8,128)(2,1)S(1)}, u32[]{:S(2)}, u32[]{:S(2)}) collective-permute-start(bf16[32,384]{1,0:T(8,128)(2,1)S(1)} %get-tuple-element.12.refs_0_), channel_id=1, source_target_pairs={{0,8},{1,9},{2,10},{3,11},{4,12},{5,13},{6,14},{7,15},{8,0},{9,1},... | collective-permute-start | bytes 73736 | tf_op jit(solution)/shard_map/ppermute | solution.py:281
  7.7 0.0 copy-start
  7.7 0.0 copy-start.1
  7.7 0.0 copy-start.2
  7.7 1.5 %green.1.refs_4_ = bf16[4,6,256,192]{3,2,1,0:T(8,128)(2,1)S(1)} custom-call(f32[4,192]{1,0:T(4,128)S(1)} %get-tuple-element.13.wave_ref, s32[2,192]{1,0:T(2,128)S(1)} %get-tuple-element.14.place_ref), custom_call_target="tpu_custom_call" | custom-call | tf_op jit(solution)/shard_map/green/pallas_call | solution.py:283
  9.2 0.0 collective-permute-done.2.refs_3_
  9.2 2.6 %collective-permute-done.1.refs_2_ = bf16[32,384]{1,0:T(8,128)(2,1)S(1)} collective-permute-done((bf16[32,384]{1,0:T(8,128)(2,1)S(1)}, bf16[32,384]{1,0:T(8,128)(2,1)S(1)}, u32[]{:S(2)}, u32[]{:S(2)}) %collective-permute-start.1) | collective-permute-done | bytes 24608 | tf_op jit(solution)/shard_map/ppermute | solution.py:281
  11.8 0.0 collective-permute-done.refs_1_
  11.8 0.7 %fields.1 = (f32[32,384]{1,0:T(8,128)S(1)}, f32[32,384]{1,0:T(8,128)S(1)}, bf16[2,32,384]{2,1,0:T(8,128)(2,1)S(1)}, bf16[32,384]{1,0:T(8,128)(2,1)S(1)}, bf16[32,384]{1,0:T(8,128)(2,1)S(1)}) custom-call(bf16[32,384]{1,0:T(8,128)(2,1)S(1)} %get-tuple-element.12.refs_0_, bf16[32,384]{1,0:T(8,128)(2,1)S(1)} %collective-permute-done.refs_1_, ...), custom_call_target="tpu_custom_call" | custom-call | tf_op jit(solution)/shard_map/fields/pallas_call | solution.py:293
  12.5 1.6 %collective-permute-start.5 = (bf16[2,32,384]{2,1,0:T(8,128)(2,1)S(1)}, bf16[2,32,384]{2,1,0:T(8,128)(2,1)S(1)}, u32[]{:S(2)}, u32[]{:S(2)}) collective-permute-start(bf16[2,32,384]{2,1,0:T(8,128)(2,1)S(1)} %get-tuple-element.18), channel_id=1, source_target_pairs={{0,4},{1,5},{2,6},{3,7},{4,0},{5,1},{6,2},{7,3},{8,12},{9,13},{10,... | collective-permute-start | bytes 147464 | tf_op jit(solution)/shard_map/ppermute | solution.py:281
  14.1 0.0 collective-permute-start.3
  14.1 1.7 %collective-permute-start.4 = (bf16[32,384]{1,0:T(8,128)(2,1)S(1)}, bf16[32,384]{1,0:T(8,128)(2,1)S(1)}, u32[]{:S(2)}, u32[]{:S(2)}) collective-permute-start(bf16[32,384]{1,0:T(8,128)(2,1)S(1)} %get-tuple-element.17), channel_id=1, source_target_pairs={{0,3},{1,2},{2,1},{3,0},{4,7},{5,6},{6,5},{7,4},{8,11},{9,10},{10,... | collective-permute-start | bytes 73736 | tf_op jit(solution)/shard_map/ppermute | solution.py:281
  15.8 0.9 %collective-permute-done.5.refs_7_ = bf16[2,32,384]{2,1,0:T(8,128)(2,1)S(1)} collective-permute-done((bf16[2,32,384]{2,1,0:T(8,128)(2,1)S(1)}, bf16[2,32,384]{2,1,0:T(8,128)(2,1)S(1)}, u32[]{:S(2)}, u32[]{:S(2)}) %collective-permute-start.5) | collective-permute-done | bytes 49184 | tf_op jit(solution)/shard_map/ppermute | solution.py:281
  16.7 0.1 collective-permute-start.6
  16.8 1.5 %collective-permute-done.3.refs_5_ = bf16[32,384]{1,0:T(8,128)(2,1)S(1)} collective-permute-done((bf16[32,384]{1,0:T(8,128)(2,1)S(1)}, bf16[32,384]{1,0:T(8,128)(2,1)S(1)}, u32[]{:S(2)}, u32[]{:S(2)}) %collective-permute-start.3) | collective-permute-done | bytes 24608 | tf_op jit(solution)/shard_map/ppermute | solution.py:281
  18.3 0.0 collective-permute-done.4.refs_6_
  18.3 0.0 collective-permute-done.6.refs_8_
  18.3 0.0 copy-done
  18.3 0.0 copy-done.1
  18.3 0.0 copy-done.2
  18.3 0.9 %finish.1 = (f32[4,2,6,4,32]{4,3,2,1,0:T(4,128)}, f32[4,2,6,4,32]{4,3,2,1,0:T(4,128)}) custom-call(s32[2,32]{1,0:T(2,128)S(1)} %copy-done.2, f32[4,4,32]{2,1,0:T(4,128)S(1)} %get-tuple-element.11.refs_1_, bf16[4,2,6,4,32]{4,3,2,1,0:T(4,128)(2,1)S(1)} %copy-done, bf16[4,2,6,4,32]{4,3,2,1,0:T(4,128)(2,1)S(1)} %copy-done.1, ...), custom_call_target="tpu_custom_call" | custom-call | tf_op jit(solution)/shard_map/finish/pallas_call | solution.py:306
  (1 shorter events, 0.0 us)
Async XLA Ops:
  1.9 7.3 %collective-permute-start.2 = (bf16[32,384]{1,0:T(8,128)(2,1)S(1)}, bf16[32,384]{1,0:T(8,128)(2,1)S(1)}, u32[]{:S(2)}, u32[]{:S(2)}) collective-permute-start(bf16[32,384]{1,0:T(8,128)(2,1)S(1)} %get-tuple-element.12.refs_0_), channel_id=1, source_target_pairs={{0,24},{1,25},{2,26},{3,27},{4,28},{5,29},{6,30},{7,31},{8,16},{9,... | collective-permute-start | bytes 73736 | tf_op jit(solution)/shard_map/ppermute | solution.py:281
  7.1 4.7 %collective-permute-start.1 = (bf16[32,384]{1,0:T(8,128)(2,1)S(1)}, bf16[32,384]{1,0:T(8,128)(2,1)S(1)}, u32[]{:S(2)}, u32[]{:S(2)}) collective-permute-start(bf16[32,384]{1,0:T(8,128)(2,1)S(1)} %get-tuple-element.12.refs_0_), channel_id=1, source_target_pairs={{0,16},{1,17},{2,18},{3,19},{4,20},{5,21},{6,22},{7,23},{8,24},{9,... | collective-permute-start | bytes 73736 | tf_op jit(solution)/shard_map/ppermute | solution.py:281
  7.1 4.7 %collective-permute-start = (bf16[32,384]{1,0:T(8,128)(2,1)S(1)}, bf16[32,384]{1,0:T(8,128)(2,1)S(1)}, u32[]{:S(2)}, u32[]{:S(2)}) collective-permute-start(bf16[32,384]{1,0:T(8,128)(2,1)S(1)} %get-tuple-element.12.refs_0_), channel_id=1, source_target_pairs={{0,8},{1,9},{2,10},{3,11},{4,12},{5,13},{6,14},{7,15},{8,0},{9,1},... | collective-permute-start | bytes 73736 | tf_op jit(solution)/shard_map/ppermute | solution.py:281
  7.7 10.6 %copy-start = (bf16[4,2,6,4,32]{4,3,2,1,0:T(4,128)(2,1)S(1)}, bf16[4,2,6,4,32]{4,3,2,1,0:T(4,128)(2,1)}, u32[]{:S(2)}) copy-start(bf16[4,2,6,4,32]{4,3,2,1,0:T(4,128)(2,1)} %refs_2_.1) | copy-start | bytes 36868
  7.7 10.6 %copy-start.1 = (bf16[4,2,6,4,32]{4,3,2,1,0:T(4,128)(2,1)S(1)}, bf16[4,2,6,4,32]{4,3,2,1,0:T(4,128)(2,1)}, u32[]{:S(2)}) copy-start(bf16[4,2,6,4,32]{4,3,2,1,0:T(4,128)(2,1)} %refs_3_.1) | copy-start | bytes 36868
  7.7 10.6 %copy-start.2 = (s32[2,32]{1,0:T(2,128)S(1)}, s32[2,32]{1,0:T(2,128)}, u32[]{:S(2)}) copy-start(s32[2,32]{1,0:T(2,128)} %refs_0_.3) | copy-start | bytes 772
  12.5 4.2 %collective-permute-start.5 = (bf16[2,32,384]{2,1,0:T(8,128)(2,1)S(1)}, bf16[2,32,384]{2,1,0:T(8,128)(2,1)S(1)}, u32[]{:S(2)}, u32[]{:S(2)}) collective-permute-start(bf16[2,32,384]{2,1,0:T(8,128)(2,1)S(1)} %get-tuple-element.18), channel_id=1, source_target_pairs={{0,4},{1,5},{2,6},{3,7},{4,0},{5,1},{6,2},{7,3},{8,12},{9,13},{10,... | collective-permute-start | bytes 147464 | tf_op jit(solution)/shard_map/ppermute | solution.py:281
  14.1 4.2 %collective-permute-start.3 = (bf16[32,384]{1,0:T(8,128)(2,1)S(1)}, bf16[32,384]{1,0:T(8,128)(2,1)S(1)}, u32[]{:S(2)}, u32[]{:S(2)}) collective-permute-start(bf16[32,384]{1,0:T(8,128)(2,1)S(1)} %get-tuple-element.16), channel_id=1, source_target_pairs={{0,7},{1,6},{2,5},{3,4},{4,3},{5,2},{6,1},{7,0},{8,15},{9,14},{10,... | collective-permute-start | bytes 73736 | tf_op jit(solution)/shard_map/ppermute | solution.py:281
  14.1 4.2 %collective-permute-start.4 = (bf16[32,384]{1,0:T(8,128)(2,1)S(1)}, bf16[32,384]{1,0:T(8,128)(2,1)S(1)}, u32[]{:S(2)}, u32[]{:S(2)}) collective-permute-start(bf16[32,384]{1,0:T(8,128)(2,1)S(1)} %get-tuple-element.17), channel_id=1, source_target_pairs={{0,3},{1,2},{2,1},{3,0},{4,7},{5,6},{6,5},{7,4},{8,11},{9,10},{10,... | collective-permute-start | bytes 73736 | tf_op jit(solution)/shard_map/ppermute | solution.py:281
  16.7 1.6 %collective-permute-start.6 = (bf16[32,384]{1,0:T(8,128)(2,1)S(1)}, bf16[32,384]{1,0:T(8,128)(2,1)S(1)}, u32[]{:S(2)}, u32[]{:S(2)}) collective-permute-start(bf16[32,384]{1,0:T(8,128)(2,1)S(1)} %fusion), channel_id=1, source_target_pairs={{0,1},{1,0},{2,3},{3,2},{4,5},{5,4},{6,7},{7,6},{8,9},{9,8},{10,11... | collective-permute-start | bytes 73736 | tf_op jit(solution)/shard_map/ppermute | solution.py:281

commit v4 on v3

--- a/solution.py
+++ b/solution.py
@@ -48,9 +48,9 @@
 def pack_kernel(*refs):
     sources, (payload_ref, alpha_ref, waves_ref, place_ref), scratch = refs[:6], refs[6:10], refs[10:]
     copies = [pltpu.make_async_copy(source, there, scratch[-1].at[i]) for i, (source, there) in enumerate(zip(sources, scratch))]
-    for copy in copies:
+    for copy in reversed(copies):
         copy.start()
-    for copy in copies:
+    for copy in copies[:4]:
         copy.wait()
     lattice_ref, material_ref, pol_ref, wave_ref, dip_ref, adj_ref = scratch[:6]
     waves, _, _, excite, atoms = dip_ref.shape
@@ -60,13 +60,23 @@
     place_ref[...] = jnp.broadcast_to(lattice_ref[:, 0:1], place_ref.shape)
     kinds = lax.broadcasted_iota(jnp.int32, (types, atoms), 0)
     onehot = jnp.where(kinds == material_ref[...], 1.0, 0.0).astype(jnp.float32)
-    alpha = []
+    rest = jnp.concatenate([pol_ref[kind] for kind in range(4)], axis=0)
+    parts = []
+    for _ in range(3):
+        part = rest.astype(jnp.bfloat16)
+        rest = rest - part.astype(jnp.float32)
+        parts.append(part)
+    onehot = onehot.astype(jnp.bfloat16)
+    table = jnp.dot(
+        jnp.concatenate(parts, axis=1),
+        jnp.concatenate([onehot] * 3, axis=0),
+        preferred_element_type=jnp.float32,
+    )
+    alpha = [table[kind * waves : (kind + 1) * waves] for kind in range(4)]
     for kind in range(4):
-        value = jnp.dot(
-            pol_ref[kind], onehot, precision=lax.Precision.HIGHEST, preferred_element_type=jnp.float32
-        )
-        alpha_ref[kind] = value
-        alpha.append(value)
+        alpha_ref[kind] = alpha[kind]
+    for copy in copies[4:]:
+        copy.wait()
     rows = []
     for w in range(waves):
         fwd = {}
@@ -99,6 +109,18 @@
     ).astype(jnp.bfloat16)
 
 
+def slot_groups(depth):
+    order = [0] + list(range(depth - 1, 0, -1))
+    half = depth // 2
+    return order[:half], order[half:]
+
+
+def kernel_row(k, part, depth):
+    for number, group in enumerate(slot_groups(depth)):
+        if k in group:
+            return (2 * number * len(group) + part * len(group) + group.index(k)) * ATOMS
+
+
 def sin_cos(x):
     turns = jnp.floor(x * 0.6366197723675814 + 0.5)
     rest = ((x - turns * 1.5703125) - turns * 4.837512969970703125e-4) - turns * 7.54978995489188216e-8
@@ -114,8 +136,7 @@
 
 
 def green_kernel(wave_ref, place_ref, out_ref, *, n_tgt, n_src):
-    waves, _, double, targets = out_ref.shape
-    sources = double // 2
+    waves, _, _, targets = out_ref.shape
     depth = n_tgt // BANDS
     band = place_ref[0:1] // TILE_X
     column = place_ref[1:2] // TILE_Y
@@ -160,7 +181,7 @@
             far = (3.0 * e_re - g_re, 3.0 * e_im - g_im)
             cross = (g_re - h_im, g_im + h_re)
             for part in range(2):
-                there = pl.ds(part * sources + k * ATOMS, ATOMS)
+                there = pl.ds(kernel_row(k, part, depth), ATOMS)
                 n, f, c = near[part], far[part], cross[part]
                 out_ref[w, 0, there] = (n + f * xx).astype(jnp.bfloat16)
                 out_ref[w, 1, there] = (n + f * yy).astype(jnp.bfloat16)
@@ -170,11 +191,12 @@
                 out_ref[w, 5, there] = (c * ux).astype(jnp.bfloat16)
 
 
-def field_kernel(*refs):
-    *tile_refs, kernels_ref, own_ref, core_ref, flip_ref, side_ref, cross_ref = refs
+def group_fields(tile_refs, kernels_ref, group):
     waves = kernels_ref.shape[0]
-    gathered = jnp.concatenate([ref[...].astype(jnp.float32) for ref in tile_refs], axis=0)
-    rows = gathered.T.astype(jnp.bfloat16)
+    count = len(tile_refs) * ATOMS
+    once = jnp.concatenate([ref[...] for ref in tile_refs], axis=0)
+    rows = jnp.concatenate([once, once], axis=0).astype(jnp.float32).T
+    first = lax.broadcasted_iota(jnp.int32, (1, 2 * count), 1) < count
     half = rows.shape[0] // (waves * 6)
     fields = []
     for w in range(waves):
@@ -182,20 +204,28 @@
         for c in range(3):
             base = (w * 3 + c) * 2 * half
             re, im = rows[base : base + half], rows[base + half : base + 2 * half]
-            left.append(
-                jnp.concatenate(
-                    [jnp.concatenate([re, -im], axis=1), jnp.concatenate([im, re], axis=1)], axis=0
-                )
-            )
+            both = [jnp.where(first, re, -im), jnp.where(first, im, re)]
+            left.append(jnp.concatenate(both, axis=0).astype(jnp.bfloat16))
         total = [None] * 3
         for index, places in enumerate(PLACES):
             stacked = jnp.concatenate([left[c_in] for c_in, _ in places], axis=0)
-            product = jnp.dot(stacked, kernels_ref[w, index], preferred_element_type=jnp.float32)
+            chosen = kernels_ref[w, index, 2 * group * count : 2 * (group + 1) * count]
+            product = jnp.dot(stacked, chosen, preferred_element_type=jnp.float32)
             for number, (_, c_out) in enumerate(places):
-                piece = product[number * 2 * half : (number + 1) * 2 * half]
-                total[c_out] = piece if total[c_out] is None else total[c_out] + piece
+                there = product[number * 2 * half : (number + 1) * 2 * half]
+                total[c_out] = there if total[c_out] is None else total[c_out] + there
         fields += total
-    turned = jnp.concatenate(fields, axis=0).T
+    return jnp.concatenate(fields, axis=0)
+
+
+def early_kernel(*refs):
+    *tile_refs, kernels_ref, sum_ref = refs
+    sum_ref[...] = group_fields(tile_refs, kernels_ref, 0)
+
+
+def late_kernel(*refs):
+    *tile_refs, kernels_ref, sum_ref, own_ref, core_ref, flip_ref, side_ref, cross_ref = refs
+    turned = (group_fields(tile_refs, kernels_ref, 1) + sum_ref[...]).T
     piece = lambda slot, flip: turned[(slot * BANDS + flip) * ATOMS :][:ATOMS]
     own_ref[...] = piece(0, 0)
     core_ref[...] = piece(1, 0)
@@ -290,14 +320,23 @@
     )(wave_rows, place)
     tile = jax.ShapeDtypeStruct((atoms, width), jnp.bfloat16)
     wide = jax.ShapeDtypeStruct((atoms, width), jnp.float32)
+    early, late = slot_groups(depth)
+    early_sum = pl.pallas_call(
+        early_kernel,
+        in_specs=vmem(len(early) + 1),
+        out_specs=pl.BlockSpec(memory_space=pltpu.VMEM),
+        out_shape=jax.ShapeDtypeStruct((width, targets), jnp.float32),
+        compiler_params=pltpu.CompilerParams(vmem_limit_bytes=12 << 20),
+        name="early",
+    )(*[tiles[k] for k in early], kernels)
     own, core, flip, side, cross = pl.pallas_call(
-        field_kernel,
-        in_specs=vmem(depth + 1),
+        late_kernel,
+        in_specs=vmem(len(late) + 2),
         out_specs=vmem(5),
         out_shape=(wide, wide, jax.ShapeDtypeStruct((2, atoms, width), jnp.bfloat16), tile, tile),
         compiler_params=pltpu.CompilerParams(vmem_limit_bytes=12 << 20),
-        name="fields",
-    )(*tiles, kernels)
+        name="late",
+    )(*[tiles[k] for k in late], kernels, early_sum)
     cross = send(cross, 0, 1, 2)
     side = send(side, 0, 0, 2)
     flip = send(flip, 0, 1, 0)

time: 19.6 us -> 19.3 us (0.985)
  waiting for transfers between devices: 4.94 us -> 4.51 us
    ppermute x7, waiting for transfers between devices: 4.94 us -> 4.51 us  [per_device(): lax.ppermute(x, AXES, pairs(n_tgt, n_src, shift, flip, slot))]
    pallas_call x1 -> x2, Pallas kernels: 0.74 us -> 0.95 us  [the longest x1 0.52 us: per_device(): pl.pallas_call(late_kernel, in_specs=vmem(len(late) + 2), out_specs=vmem(...]
  transfers between devices with their start and end apart: 7 -> 7, of which waited for: 3 -> 4; matrix products, arithmetic and copies ran while one was open for 0% -> 0% of each run, Pallas kernels for 8% -> 10%
where the time goes in v4:
time: 19.3 us; the launch traced here: 19 us
  starting transfers between devices  9.13 us (47%)
  Pallas kernels  4.59 us (24%)
  waiting for transfers between devices  4.51 us (23%)
  between operations  0.72 us (4%)
    ppermute x7, starting transfers between devices, per_device(): lax.ppermute(x, AXES, pairs(n_tgt, n_src, shift, flip, slot))  9.13 us
    ppermute x7, waiting for transfers between devices, per_device(): lax.ppermute(x, AXES, pairs(n_tgt, n_src, shift, flip, slot))  4.51 us
    pallas_call x1, Pallas kernels, per_device(): pl.pallas_call(functools.partial(green_kernel, n_tgt=n_tgt, n_src=n_src),...  1.49 us
    pallas_call x1, Pallas kernels, per_device(): pl.pallas_call(pack_kernel, in_specs=[pl.BlockSpec(memory_space=pltpu.HBM...  1.22 us
    pallas_call x1, Pallas kernels, per_device(): pl.pallas_call(finish_kernel, in_specs=vmem(5 + len(got)), out_specs=vmem...  0.93 us
    pallas_call x1, Pallas kernels, per_device(): pl.pallas_call(late_kernel, in_specs=vmem(len(late) + 2), out_specs=vmem(...  0.52 us
    pallas_call x1, Pallas kernels, per_device(): pl.pallas_call(early_kernel, in_specs=vmem(len(early) + 1), out_specs=pl....  0.43 us
  transfers between devices with their start and end apart: 7, of which 4 were waited for; matrix products, arithmetic and copies ran while one was open for 0% of the time, Pallas kernels for 10%

profile of v4, /device:TPU:0, one launch (start us, length us, event | category | flops | bytes accessed | tf_op | source)
XLA Modules:
  0.0 19.0 jit_solution(14637085746717451492)
XLA Ops:
  0.6 1.2 %pack.1 = (bf16[32,384]{1,0:T(8,128)(2,1)S(1)}, f32[4,4,32]{2,1,0:T(4,128)S(1)}, f32[4,192]{1,0:T(4,128)S(1)}, s32[2,192]{1,0:T(2,128)S(1)}) custom-call(s32[2,32]{1,0:T(2,128)} %refs_0_.3, s32[1,32]{1,0:T(1,128)} %bitcast.9, f32[4,4,16]{2,1,0:T(4,128)} %bitcast.8, f32[1,4]{1,0:T(1,128)} %bitcast.10, bf16[4,2,6,4,32]{4,3,2,1,0:T(4,128)(2,1)} %refs_2_.1, ...), custom_call_target="tpu_custom_call" | custom-call | tf_op jit(solution)/shard_map/pack/pallas_call | solution.py:296
  1.9 5.1 %collective-permute-start.2 = (bf16[32,384]{1,0:T(8,128)(2,1)S(1)}, bf16[32,384]{1,0:T(8,128)(2,1)S(1)}, u32[]{:S(2)}, u32[]{:S(2)}) collective-permute-start(bf16[32,384]{1,0:T(8,128)(2,1)S(1)} %get-tuple-element.12.refs_0_), channel_id=1, source_target_pairs={{0,24},{1,25},{2,26},{3,27},{4,28},{5,29},{6,30},{7,31},{8,16},{9,... | collective-permute-start | bytes 73736 | tf_op jit(solution)/shard_map/ppermute | solution.py:311
  7.0 0.0 collective-permute-start.1
  7.0 0.6 %collective-permute-start = (bf16[32,384]{1,0:T(8,128)(2,1)S(1)}, bf16[32,384]{1,0:T(8,128)(2,1)S(1)}, u32[]{:S(2)}, u32[]{:S(2)}) collective-permute-start(bf16[32,384]{1,0:T(8,128)(2,1)S(1)} %get-tuple-element.12.refs_0_), channel_id=1, source_target_pairs={{0,16},{1,17},{2,18},{3,19},{4,20},{5,21},{6,22},{7,23},{8,24},{9,... | collective-permute-start | bytes 73736 | tf_op jit(solution)/shard_map/ppermute | solution.py:311
  7.6 1.5 %green.1.refs_2_ = bf16[4,6,256,192]{3,2,1,0:T(8,128)(2,1)S(1)} custom-call(f32[4,192]{1,0:T(4,128)S(1)} %get-tuple-element.13.wave_ref, s32[2,192]{1,0:T(2,128)S(1)} %get-tuple-element.14.place_ref), custom_call_target="tpu_custom_call" | custom-call | tf_op jit(solution)/shard_map/green/pallas_call | solution.py:313
  9.1 0.0 copy-start
  9.2 0.0 copy-start.1
  9.2 0.0 copy-start.2
  9.2 0.0 collective-permute-done.2.refs_1_
  9.2 0.4 %early.1.refs_3_ = f32[384,192]{1,0:T(8,128)S(1)} custom-call(bf16[32,384]{1,0:T(8,128)(2,1)S(1)} %get-tuple-element.12.refs_0_, bf16[32,384]{1,0:T(8,128)(2,1)S(1)} %collective-permute-done.2.refs_1_, bf16[4,6,256,192]{3,2,1,0:T(8,128)(2,1)S(1)} %green.1.refs_2_), custom_call_target="tpu_custom_call" | custom-call | tf_op jit(solution)/shard_map/early/pallas_call | solution.py:324
  9.6 1.2 %collective-permute-done.1.refs_1_ = bf16[32,384]{1,0:T(8,128)(2,1)S(1)} collective-permute-done((bf16[32,384]{1,0:T(8,128)(2,1)S(1)}, bf16[32,384]{1,0:T(8,128)(2,1)S(1)}, u32[]{:S(2)}, u32[]{:S(2)}) %collective-permute-start.1) | collective-permute-done | bytes 24608 | tf_op jit(solution)/shard_map/ppermute | solution.py:311
  10.8 0.9 %collective-permute-done.refs_0_ = bf16[32,384]{1,0:T(8,128)(2,1)S(1)} collective-permute-done((bf16[32,384]{1,0:T(8,128)(2,1)S(1)}, bf16[32,384]{1,0:T(8,128)(2,1)S(1)}, u32[]{:S(2)}, u32[]{:S(2)}) %collective-permute-start) | collective-permute-done | bytes 24608 | tf_op jit(solution)/shard_map/ppermute | solution.py:311
  11.8 0.5 %late.1 = (f32[32,384]{1,0:T(8,128)S(1)}, f32[32,384]{1,0:T(8,128)S(1)}, bf16[2,32,384]{2,1,0:T(8,128)(2,1)S(1)}, bf16[32,384]{1,0:T(8,128)(2,1)S(1)}, bf16[32,384]{1,0:T(8,128)(2,1)S(1)}) custom-call(bf16[32,384]{1,0:T(8,128)(2,1)S(1)} %collective-permute-done.refs_0_, bf16[32,384]{1,0:T(8,128)(2,1)S(1)} %collective-permute-done.1.refs_1_, ...), custom_call_target="tpu_custom_call" | custom-call | tf_op jit(solution)/shard_map/late/pallas_call | solution.py:332
  12.3 1.6 %collective-permute-start.5 = (bf16[2,32,384]{2,1,0:T(8,128)(2,1)S(1)}, bf16[2,32,384]{2,1,0:T(8,128)(2,1)S(1)}, u32[]{:S(2)}, u32[]{:S(2)}) collective-permute-start(bf16[2,32,384]{2,1,0:T(8,128)(2,1)S(1)} %get-tuple-element.18), channel_id=1, source_target_pairs={{0,4},{1,5},{2,6},{3,7},{4,0},{5,1},{6,2},{7,3},{8,12},{9,13},{10,... | collective-permute-start | bytes 147464 | tf_op jit(solution)/shard_map/ppermute | solution.py:311
  13.9 0.0 collective-permute-start.3
  13.9 1.7 %collective-permute-start.4 = (bf16[32,384]{1,0:T(8,128)(2,1)S(1)}, bf16[32,384]{1,0:T(8,128)(2,1)S(1)}, u32[]{:S(2)}, u32[]{:S(2)}) collective-permute-start(bf16[32,384]{1,0:T(8,128)(2,1)S(1)} %get-tuple-element.17), channel_id=1, source_target_pairs={{0,3},{1,2},{2,1},{3,0},{4,7},{5,6},{6,5},{7,4},{8,11},{9,10},{10,... | collective-permute-start | bytes 73736 | tf_op jit(solution)/shard_map/ppermute | solution.py:311
  15.6 0.9 %collective-permute-done.5.refs_7_ = bf16[2,32,384]{2,1,0:T(8,128)(2,1)S(1)} collective-permute-done((bf16[2,32,384]{2,1,0:T(8,128)(2,1)S(1)}, bf16[2,32,384]{2,1,0:T(8,128)(2,1)S(1)}, u32[]{:S(2)}, u32[]{:S(2)}) %collective-permute-start.5) | collective-permute-done | bytes 49184 | tf_op jit(solution)/shard_map/ppermute | solution.py:311
  16.4 0.1 collective-permute-start.6
  16.5 1.5 %collective-permute-done.3.refs_5_ = bf16[32,384]{1,0:T(8,128)(2,1)S(1)} collective-permute-done((bf16[32,384]{1,0:T(8,128)(2,1)S(1)}, bf16[32,384]{1,0:T(8,128)(2,1)S(1)}, u32[]{:S(2)}, u32[]{:S(2)}) %collective-permute-start.3) | collective-permute-done | bytes 24608 | tf_op jit(solution)/shard_map/ppermute | solution.py:311
  18.0 0.0 collective-permute-done.4.refs_6_
  18.0 0.0 collective-permute-done.6.refs_8_
  18.0 0.0 copy-done
  18.0 0.0 copy-done.1
  18.0 0.0 copy-done.2
  18.0 0.9 %finish.1 = (f32[4,2,6,4,32]{4,3,2,1,0:T(4,128)}, f32[4,2,6,4,32]{4,3,2,1,0:T(4,128)}) custom-call(s32[2,32]{1,0:T(2,128)S(1)} %copy-done.2, f32[4,4,32]{2,1,0:T(4,128)S(1)} %get-tuple-element.11.refs_1_, bf16[4,2,6,4,32]{4,3,2,1,0:T(4,128)(2,1)S(1)} %copy-done, bf16[4,2,6,4,32]{4,3,2,1,0:T(4,128)(2,1)S(1)} %copy-done.1, ...), custom_call_target="tpu_custom_call" | custom-call | tf_op jit(solution)/shard_map/finish/pallas_call | solution.py:345
  (1 shorter events, 0.0 us)
Async XLA Ops:
  1.9 7.3 %collective-permute-start.2 = (bf16[32,384]{1,0:T(8,128)(2,1)S(1)}, bf16[32,384]{1,0:T(8,128)(2,1)S(1)}, u32[]{:S(2)}, u32[]{:S(2)}) collective-permute-start(bf16[32,384]{1,0:T(8,128)(2,1)S(1)} %get-tuple-element.12.refs_0_), channel_id=1, source_target_pairs={{0,24},{1,25},{2,26},{3,27},{4,28},{5,29},{6,30},{7,31},{8,16},{9,... | collective-permute-start | bytes 73736 | tf_op jit(solution)/shard_map/ppermute | solution.py:311
  7.0 3.8 %collective-permute-start.1 = (bf16[32,384]{1,0:T(8,128)(2,1)S(1)}, bf16[32,384]{1,0:T(8,128)(2,1)S(1)}, u32[]{:S(2)}, u32[]{:S(2)}) collective-permute-start(bf16[32,384]{1,0:T(8,128)(2,1)S(1)} %get-tuple-element.12.refs_0_), channel_id=1, source_target_pairs={{0,8},{1,9},{2,10},{3,11},{4,12},{5,13},{6,14},{7,15},{8,0},{9,1},... | collective-permute-start | bytes 73736 | tf_op jit(solution)/shard_map/ppermute | solution.py:311
  7.0 4.8 %collective-permute-start = (bf16[32,384]{1,0:T(8,128)(2,1)S(1)}, bf16[32,384]{1,0:T(8,128)(2,1)S(1)}, u32[]{:S(2)}, u32[]{:S(2)}) collective-permute-start(bf16[32,384]{1,0:T(8,128)(2,1)S(1)} %get-tuple-element.12.refs_0_), channel_id=1, source_target_pairs={{0,16},{1,17},{2,18},{3,19},{4,20},{5,21},{6,22},{7,23},{8,24},{9,... | collective-permute-start | bytes 73736 | tf_op jit(solution)/shard_map/ppermute | solution.py:311
  9.1 8.9 %copy-start = (bf16[4,2,6,4,32]{4,3,2,1,0:T(4,128)(2,1)S(1)}, bf16[4,2,6,4,32]{4,3,2,1,0:T(4,128)(2,1)}, u32[]{:S(2)}) copy-start(bf16[4,2,6,4,32]{4,3,2,1,0:T(4,128)(2,1)} %refs_2_.1) | copy-start | bytes 36868
  9.2 8.9 %copy-start.1 = (bf16[4,2,6,4,32]{4,3,2,1,0:T(4,128)(2,1)S(1)}, bf16[4,2,6,4,32]{4,3,2,1,0:T(4,128)(2,1)}, u32[]{:S(2)}) copy-start(bf16[4,2,6,4,32]{4,3,2,1,0:T(4,128)(2,1)} %refs_3_.1) | copy-start | bytes 36868
  9.2 8.9 %copy-start.2 = (s32[2,32]{1,0:T(2,128)S(1)}, s32[2,32]{1,0:T(2,128)}, u32[]{:S(2)}) copy-start(s32[2,32]{1,0:T(2,128)} %refs_0_.3) | copy-start | bytes 772
  12.3 4.2 %collective-permute-start.5 = (bf16[2,32,384]{2,1,0:T(8,128)(2,1)S(1)}, bf16[2,32,384]{2,1,0:T(8,128)(2,1)S(1)}, u32[]{:S(2)}, u32[]{:S(2)}) collective-permute-start(bf16[2,32,384]{2,1,0:T(8,128)(2,1)S(1)} %get-tuple-element.18), channel_id=1, source_target_pairs={{0,4},{1,5},{2,6},{3,7},{4,0},{5,1},{6,2},{7,3},{8,12},{9,13},{10,... | collective-permute-start | bytes 147464 | tf_op jit(solution)/shard_map/ppermute | solution.py:311
  13.9 4.2 %collective-permute-start.3 = (bf16[32,384]{1,0:T(8,128)(2,1)S(1)}, bf16[32,384]{1,0:T(8,128)(2,1)S(1)}, u32[]{:S(2)}, u32[]{:S(2)}) collective-permute-start(bf16[32,384]{1,0:T(8,128)(2,1)S(1)} %get-tuple-element.16), channel_id=1, source_target_pairs={{0,7},{1,6},{2,5},{3,4},{4,3},{5,2},{6,1},{7,0},{8,15},{9,14},{10,... | collective-permute-start | bytes 73736 | tf_op jit(solution)/shard_map/ppermute | solution.py:311
  13.9 4.2 %collective-permute-start.4 = (bf16[32,384]{1,0:T(8,128)(2,1)S(1)}, bf16[32,384]{1,0:T(8,128)(2,1)S(1)}, u32[]{:S(2)}, u32[]{:S(2)}) collective-permute-start(bf16[32,384]{1,0:T(8,128)(2,1)S(1)} %get-tuple-element.17), channel_id=1, source_target_pairs={{0,3},{1,2},{2,1},{3,0},{4,7},{5,6},{6,5},{7,4},{8,11},{9,10},{10,... | collective-permute-start | bytes 73736 | tf_op jit(solution)/shard_map/ppermute | solution.py:311
  16.4 1.6 %collective-permute-start.6 = (bf16[32,384]{1,0:T(8,128)(2,1)S(1)}, bf16[32,384]{1,0:T(8,128)(2,1)S(1)}, u32[]{:S(2)}, u32[]{:S(2)}) collective-permute-start(bf16[32,384]{1,0:T(8,128)(2,1)S(1)} %fusion), channel_id=1, source_target_pairs={{0,1},{1,0},{2,3},{3,2},{4,5},{5,4},{6,7},{7,6},{8,9},{9,8},{10,11... | collective-permute-start | bytes 73736 | tf_op jit(solution)/shard_map/ppermute | solution.py:311
